TPU v7x, 32 devices: a whole 2x2x4 slice. The times are simulated.
32 devices in a mesh: dp: 16 (over z, y, x), tensor: 2 (over core).
Axes of the slice: x: 2, y: 2, z: 4, core: 2. Of those that a mesh axis runs over, the one named last changes fastest.
Arguments:
- tokens: bfloat16 [18432, 768], P(('dp', 'tensor')), may hold values from -6 to 6
- ln1_gain: bfloat16 [768], replicated, may hold values from 0.5 to 1.5
- ln1_bias: bfloat16 [768], replicated, may hold values from -1.75 to 1.75
- qkv_weight: bfloat16 [3, 768, 768], P(None, None, 'tensor'), may hold values from -0.3125 to 0.3125
- qv_bias: bfloat16 [2, 768], P(None, 'tensor'), may hold values from -1.75 to 1.75
- out_weight: bfloat16 [768, 768], P('tensor'), may hold values from -0.625 to 0.625
- out_bias: bfloat16 [768], replicated, may hold values from -1.75 to 1.75
- ln2_gain: bfloat16 [768], replicated, may hold values from 0.5 to 1.5
- ln2_bias: bfloat16 [768], replicated, may hold values from -1.75 to 1.75
- fc_weight: bfloat16 [768, 3072], P(None, 'tensor'), may hold values from -0.21875 to 0.21875
- fc_bias: bfloat16 [3072], P('tensor'), may hold values from -3 to 3
- proj_weight: bfloat16 [3072, 768], P('tensor'), may hold values from -0.15625 to 0.15625
- proj_bias: bfloat16 [768], replicated, may hold values from -1.75 to 1.75
- cotangent: bfloat16 [18432, 768], P(('dp', 'tensor')), may hold values from -6 to 6
Outputs:
- block_output: bfloat16 [18432, 768], P(('dp', 'tensor'))
- input_grad: bfloat16 [18432, 768], P(('dp', 'tensor'))
- grad_ln1_gain: float32 [768], replicated
- grad_ln1_bias: float32 [768], replicated
- grad_qkv_weight: float32 [3, 768, 768], P(None, None, 'tensor')
- grad_qv_bias: float32 [2, 768], P(None, 'tensor')
- grad_out_weight: float32 [768, 768], P('tensor')
- grad_out_bias: float32 [768], replicated
- grad_ln2_gain: float32 [768], replicated
- grad_ln2_bias: float32 [768], replicated
- grad_fc_weight: float32 [768, 3072], P(None, 'tensor')
- grad_fc_bias: float32 [3072], P('tensor')
- grad_proj_weight: float32 [3072, 768], P('tensor')
- grad_proj_bias: float32 [768], replicated
All inputs are finite; a program needn't handle non-finite values.
Results may differ from a plain program's by a relative error of at most 0.014.
The roundings to bfloat16 on the way count: a program that leaves them out, or rounds other values in their place, can miss the bound.
Values may be sent and summed in bfloat16 or wider, within the bound.
A program may use at most 192 MiB of HBM per device.

v0:
```python
import jax
import jax.numpy as jnp
from jax import lax
from jax.sharding import PartitionSpec as P

HD = 64
PROMPT = 896
CONT = 128
NCONT = 2


EPSILON = 1e-05
MASKED = -1e30


def norm_rows(values, gain_vec, shift_vec):
    mean_row = jnp.mean(values, axis=-1, keepdims=True)
    centred = values - mean_row
    inv_std = lax.rsqrt(jnp.mean(centred * centred, axis=-1, keepdims=True) + EPSILON)
    normal = centred * inv_std
    return (normal * gain_vec + shift_vec, normal, inv_std)


def norm_back(grad_out, normal, inv_std, gain_vec):
    scaled = grad_out * gain_vec
    inner = (
        scaled
        - jnp.mean(scaled, axis=-1, keepdims=True)
        - normal * jnp.mean(scaled * normal, axis=-1, keepdims=True)
    )
    return inner * inv_std


def split_group(values):
    head_part = values[:PROMPT]
    tail_part = values[PROMPT:].reshape(NCONT, CONT, values.shape[1], values.shape[2])
    return (head_part, tail_part)


def causal_mask(length):
    row_pos = lax.broadcasted_iota(jnp.int32, (length, length), 0)
    col_pos = lax.broadcasted_iota(jnp.int32, (length, length), 1)
    return col_pos <= row_pos


def prompt_scores(q_head, k_head):
    scores = jnp.einsum(
        "qha,kha->hqk", q_head, k_head, preferred_element_type=jnp.float32
    ) * HD ** (-0.5)
    return jnp.where(causal_mask(PROMPT), scores, MASKED)


def tail_scores(q_tail, k_head, k_tail):
    far_scores = jnp.einsum(
        "ncha,kha->nhck", q_tail, k_head, preferred_element_type=jnp.float32
    ) * HD ** (-0.5)
    near_scores = jnp.einsum(
        "ncha,ndha->nhcd", q_tail, k_tail, preferred_element_type=jnp.float32
    ) * HD ** (-0.5)
    return (far_scores, jnp.where(causal_mask(CONT), near_scores, MASKED))


def attend_forward(queries, keys_all, values):
    q_head, q_tail = split_group(queries)
    k_head, k_tail = split_group(keys_all)
    v_head, v_tail = split_group(values)
    scores = prompt_scores(q_head, k_head)
    top_head = jnp.max(scores, axis=-1, keepdims=True)
    expo_head = jnp.exp(scores - top_head)
    total_head = jnp.sum(expo_head, axis=-1, keepdims=True)
    prob_head = (expo_head / total_head).astype(jnp.bfloat16)
    lse_head = top_head + jnp.log(total_head)
    out_head = jnp.einsum("hqk,kha->qha", prob_head, v_head, preferred_element_type=jnp.float32)
    far_scores, near_scores = tail_scores(q_tail, k_head, k_tail)
    top_tail = jnp.maximum(
        jnp.max(far_scores, axis=-1, keepdims=True), jnp.max(near_scores, axis=-1, keepdims=True)
    )
    expo_far = jnp.exp(far_scores - top_tail)
    expo_near = jnp.exp(near_scores - top_tail)
    total_tail = jnp.sum(expo_far, axis=-1, keepdims=True) + jnp.sum(
        expo_near, axis=-1, keepdims=True
    )
    prob_far = (expo_far / total_tail).astype(jnp.bfloat16)
    prob_near = (expo_near / total_tail).astype(jnp.bfloat16)
    lse_tail = top_tail + jnp.log(total_tail)
    out_tail = jnp.einsum("nhck,kha->ncha", prob_far, v_head, preferred_element_type=jnp.float32)
    out_tail = out_tail + jnp.einsum(
        "nhcd,ndha->ncha", prob_near, v_tail, preferred_element_type=jnp.float32
    )
    heads_local = queries.shape[1]
    mixed = jnp.concatenate([out_head, out_tail.reshape(NCONT * CONT, heads_local, HD)], axis=0)
    return (mixed, lse_head, lse_tail)


def attend_back(queries, keys_all, values, grad_mixed, lse_head, lse_tail):
    q_head, q_tail = split_group(queries)
    k_head, k_tail = split_group(keys_all)
    v_head, v_tail = split_group(values)
    g_head, g_tail = split_group(grad_mixed)
    score_scale = HD ** (-0.5)
    prob_head = jnp.exp(prompt_scores(q_head, k_head) - lse_head)
    dprob_head = jnp.einsum("qha,kha->hqk", g_head, v_head, preferred_element_type=jnp.float32)
    row_dot = jnp.sum(prob_head * dprob_head, axis=-1, keepdims=True)
    dscore_head = (prob_head * (dprob_head - row_dot)).astype(jnp.bfloat16)
    dq_head = (
        jnp.einsum("hqk,kha->qha", dscore_head, k_head, preferred_element_type=jnp.float32)
        * score_scale
    )
    dk_head = (
        jnp.einsum("hqk,qha->kha", dscore_head, q_head, preferred_element_type=jnp.float32)
        * score_scale
    )
    dv_head = jnp.einsum(
        "hqk,qha->kha", prob_head.astype(jnp.bfloat16), g_head, preferred_element_type=jnp.float32
    )
    far_scores, near_scores = tail_scores(q_tail, k_head, k_tail)
    prob_far = jnp.exp(far_scores - lse_tail)
    prob_near = jnp.exp(near_scores - lse_tail)
    dprob_far = jnp.einsum("ncha,kha->nhck", g_tail, v_head, preferred_element_type=jnp.float32)
    dprob_near = jnp.einsum("ncha,ndha->nhcd", g_tail, v_tail, preferred_element_type=jnp.float32)
    tail_dot = jnp.sum(prob_far * dprob_far, axis=-1, keepdims=True) + jnp.sum(
        prob_near * dprob_near, axis=-1, keepdims=True
    )
    dscore_far = (prob_far * (dprob_far - tail_dot)).astype(jnp.bfloat16)
    dscore_near = (prob_near * (dprob_near - tail_dot)).astype(jnp.bfloat16)
    dq_tail = jnp.einsum("nhck,kha->ncha", dscore_far, k_head, preferred_element_type=jnp.float32)
    dq_tail = (
        dq_tail
        + jnp.einsum("nhcd,ndha->ncha", dscore_near, k_tail, preferred_element_type=jnp.float32)
    ) * score_scale
    dk_head = (
        dk_head
        + jnp.einsum("nhck,ncha->kha", dscore_far, q_tail, preferred_element_type=jnp.float32)
        * score_scale
    )
    dk_tail = (
        jnp.einsum("nhcd,ncha->ndha", dscore_near, q_tail, preferred_element_type=jnp.float32)
        * score_scale
    )
    dv_head = dv_head + jnp.einsum(
        "nhck,ncha->kha", prob_far.astype(jnp.bfloat16), g_tail, preferred_element_type=jnp.float32
    )
    dv_tail = jnp.einsum(
        "nhcd,ncha->ndha",
        prob_near.astype(jnp.bfloat16),
        g_tail,
        preferred_element_type=jnp.float32,
    )
    heads_local = queries.shape[1]
    tail_rows = NCONT * CONT
    grad_query = jnp.concatenate([dq_head, dq_tail.reshape(tail_rows, heads_local, HD)], axis=0)
    grad_key = jnp.concatenate([dk_head, dk_tail.reshape(tail_rows, heads_local, HD)], axis=0)
    grad_value = jnp.concatenate([dv_head, dv_tail.reshape(tail_rows, heads_local, HD)], axis=0)
    return (grad_query, grad_key, grad_value)


def on_device(
    tokens,
    ln1_gain,
    ln1_bias,
    qkv_weight,
    qv_bias,
    out_weight,
    out_bias,
    ln2_gain,
    ln2_bias,
    fc_weight,
    fc_bias,
    proj_weight,
    proj_bias,
    cotangent,
):
    own_rows = tokens.shape[0]
    group_rows = own_rows * lax.axis_size("tensor")
    local_width = qkv_weight.shape[2]
    heads_local = local_width // HD
    gain_one = ln1_gain.astype(jnp.float32)
    gain_two = ln2_gain.astype(jnp.float32)
    x_own = tokens.astype(jnp.float32)
    normed1, normal1, inv_std1 = norm_rows(x_own, gain_one, ln1_bias.astype(jnp.float32))
    ln1_full = lax.all_gather(normed1.astype(jnp.bfloat16), "tensor", axis=0, tiled=True)
    projected = jnp.einsum("gd,tdj->gtj", ln1_full, qkv_weight, preferred_element_type=jnp.float32)
    bias_float = qv_bias.astype(jnp.float32)
    bias_rows = jnp.stack([bias_float[0], jnp.zeros_like(bias_float[0]), bias_float[1]])
    projected = (projected + bias_rows).astype(jnp.bfloat16)
    queries = projected[:, 0].reshape(group_rows, heads_local, HD)
    keys_all = projected[:, 1].reshape(group_rows, heads_local, HD)
    values = projected[:, 2].reshape(group_rows, heads_local, HD)
    mixed, lse_head, lse_tail = attend_forward(queries, keys_all, values)
    mixed_low = mixed.reshape(group_rows, local_width).astype(jnp.bfloat16)
    part_rows = mixed_low
    attn_own = lax.psum_scatter(
        jnp.dot(part_rows, out_weight, preferred_element_type=jnp.float32),
        "tensor",
        scatter_dimension=0,
        tiled=True,
    ) + out_bias.astype(jnp.float32)
    residual = x_own + attn_own
    normed2, normal2, inv_std2 = norm_rows(residual, gain_two, ln2_bias.astype(jnp.float32))
    ln2_full = lax.all_gather(normed2.astype(jnp.bfloat16), "tensor", axis=0, tiled=True)
    pre_act = jnp.dot(ln2_full, fc_weight, preferred_element_type=jnp.float32) + fc_bias.astype(
        jnp.float32
    )
    activation, gelu_pull = jax.vjp(lambda inner: jax.nn.gelu(inner, approximate=True), pre_act)
    act_low = activation.astype(jnp.bfloat16)
    part_rows = act_low
    mlp_own = lax.psum_scatter(
        jnp.dot(part_rows, proj_weight, preferred_element_type=jnp.float32),
        "tensor",
        scatter_dimension=0,
        tiled=True,
    ) + proj_bias.astype(jnp.float32)
    block_output = (residual + mlp_own).astype(jnp.bfloat16)
    cot_full = lax.all_gather(cotangent, "tensor", axis=0, tiled=True)
    grad_proj_bias = jnp.sum(cot_full, axis=0, dtype=jnp.float32)
    grad_proj_weight = jnp.einsum(
        "gf,gd->fd", act_low, cot_full, preferred_element_type=jnp.float32
    )
    grad_act = jnp.einsum("gd,fd->gf", cot_full, proj_weight, preferred_element_type=jnp.float32)
    grad_pre = gelu_pull(grad_act)[0].astype(jnp.bfloat16)
    grad_fc_bias = jnp.sum(grad_pre, axis=0, dtype=jnp.float32)
    grad_fc_weight = jnp.einsum("gd,gf->df", ln2_full, grad_pre, preferred_element_type=jnp.float32)
    part_rows = grad_pre
    grad_norm2 = lax.psum_scatter(
        jnp.einsum("gf,df->gd", part_rows, fc_weight, preferred_element_type=jnp.float32),
        "tensor",
        scatter_dimension=0,
        tiled=True,
    )
    grad_resid = cotangent.astype(jnp.float32) + norm_back(grad_norm2, normal2, inv_std2, gain_two)
    part_ln2_gain = jnp.sum(grad_norm2 * normal2, axis=0)
    part_ln2_bias = jnp.sum(grad_norm2, axis=0)
    attn_cot_full = lax.all_gather(grad_resid.astype(jnp.bfloat16), "tensor", axis=0, tiled=True)
    grad_out_bias = jnp.sum(attn_cot_full, axis=0, dtype=jnp.float32)
    grad_out_weight = jnp.einsum(
        "gj,gd->jd", mixed_low, attn_cot_full, preferred_element_type=jnp.float32
    )
    grad_mixed = jnp.einsum(
        "gd,jd->gj", attn_cot_full, out_weight, preferred_element_type=jnp.float32
    )
    grad_mixed = grad_mixed.astype(jnp.bfloat16).reshape(group_rows, heads_local, HD)
    grad_query, grad_key, grad_value = attend_back(
        queries, keys_all, values, grad_mixed, lse_head, lse_tail
    )
    grad_proj_all = (
        jnp.stack([grad_query, grad_key, grad_value], axis=1)
        .reshape(group_rows, 3, local_width)
        .astype(jnp.bfloat16)
    )
    grad_qkv_weight = jnp.einsum(
        "gd,gtj->tdj", ln1_full, grad_proj_all, preferred_element_type=jnp.float32
    )
    grad_qv_bias = jnp.sum(grad_proj_all[:, 0::2], axis=0, dtype=jnp.float32)
    part_rows = grad_proj_all
    grad_norm1 = lax.psum_scatter(
        jnp.einsum("gtj,tdj->gd", part_rows, qkv_weight, preferred_element_type=jnp.float32),
        "tensor",
        scatter_dimension=0,
        tiled=True,
    )
    input_grad = (grad_resid + norm_back(grad_norm1, normal1, inv_std1, gain_one)).astype(
        jnp.bfloat16
    )
    part_ln1_gain = jnp.sum(grad_norm1 * normal1, axis=0)
    part_ln1_bias = jnp.sum(grad_norm1, axis=0)
    grad_ln1_gain, grad_ln1_bias, grad_ln2_gain, grad_ln2_bias = lax.psum(
        (part_ln1_gain, part_ln1_bias, part_ln2_gain, part_ln2_bias), ("dp", "tensor")
    )
    summed = lax.psum(
        (
            grad_qkv_weight,
            grad_qv_bias,
            grad_out_weight,
            grad_out_bias,
            grad_fc_weight,
            grad_fc_bias,
            grad_proj_weight,
            grad_proj_bias,
        ),
        "dp",
    )
    grad_qkv_weight, grad_qv_bias, grad_out_weight, grad_out_bias = (
        summed[0],
        summed[1],
        summed[2],
        summed[3],
    )
    grad_fc_weight, grad_fc_bias, grad_proj_weight, grad_proj_bias = (
        summed[4],
        summed[5],
        summed[6],
        summed[7],
    )
    return (
        block_output,
        input_grad,
        grad_ln1_gain,
        grad_ln1_bias,
        grad_qkv_weight,
        grad_qv_bias,
        grad_out_weight,
        grad_out_bias,
        grad_ln2_gain,
        grad_ln2_bias,
        grad_fc_weight,
        grad_fc_bias,
        grad_proj_weight,
        grad_proj_bias,
    )


def solution(mesh):
    return jax.shard_map(
        on_device,
        mesh=mesh,
        in_specs=(
            P(("dp", "tensor"), None),
            P(),
            P(),
            P(None, None, "tensor"),
            P(None, "tensor"),
            P("tensor", None),
            P(),
            P(),
            P(),
            P(None, "tensor"),
            P("tensor"),
            P("tensor", None),
            P(),
            P(("dp", "tensor"), None),
        ),
        out_specs=(
            P(("dp", "tensor"), None),
            P(("dp", "tensor"), None),
            P(),
            P(),
            P(None, None, "tensor"),
            P(None, "tensor"),
            P("tensor", None),
            P(),
            P(),
            P(),
            P(None, "tensor"),
            P("tensor"),
            P("tensor", None),
            P(),
        ),
        check_vma=False,
    )
```

profile of v0, /device:TPU:0, one launch (start us, length us, event | category | flops | bytes accessed | tf_op | source)
XLA Modules:
  0.0 703.9 jit_solution(14144970885692811731)
XLA Ops:
  11.8 2.5 fusion.32
  15.6 11.6 %all-gather.5.cloned.1.call-done = bf16[1152,768]{1,0:T(8,128)(2,1)} async-done(((bf16[576,768]{1,0:T(8,128)(2,1)}), bf16[1152,768]{1,0:T(8,128)(2,1)}) %all-gather.5.cloned.1.call-update) | async-done | bytes 1769488 | tf_op jit(solution)/shard_map/all_gather | solution.py:181
  27.2 4.5 add_convert_fusion
  42.2 8.8 %fusion.102 = (f32[6,896]{1,0:T(8,128)S(1)}, f32[6,896,896]{1,2,0:T(8,128)}) fusion(bf16[896,6,64]{0,2,1:T(8,128)(2,1)S(1)} %bitcast.167, bf16[896,6,64]{0,2,1:T(8,128)(2,1)S(1)} %bitcast.164, pred[896,896]{0,1:T(8,128)(4,1)S(1)} %copy-done.18), kind=kOutput, calls=%fused_computation.160 | convolution fusion | flops 631008000 | bytes 21468160 | tf_op jit(solution)/shard_map/qha,kha->hqk/dot_general | solution.py:47
  51.1 9.1 %fusion = f32[6,896]{1,0:T(8,128)S(1)} fusion(f32[6,896,896]{1,2,0:T(8,128)} %get-tuple-element.112, f32[6,896]{1,0:T(8,128)S(1)} %get-tuple-element.111), kind=kLoop, calls=%fused_computation.6 | loop fusion | flops 9628416 | bytes 19310592 | tf_op jit(solution)/shard_map/reduce_sum | solution.py:70
  60.2 10.0 %fusion.55 = bf16[6,64,896]{2,1,0:T(8,128)(2,1)S(1)} fusion(bf16[896,6,64]{0,2,1:T(8,128)(2,1)S(1)} %bitcast.172, f32[6,896,896]{1,2,0:T(8,128)} %get-tuple-element.112, f32[6,896]{1,0:T(8,128)S(1)} %fusion, f32[6,896]{1,0:T(8,128)S(1)} %get-tuple-element.111), kind=kOutput, calls=%fused_computation.87 | convolution fusion | flops 631357440 | bytes 20686848 | tf_op jit(solution)/shard_map/hqk,kha->qha/dot_general | solution.py:73
  71.1 2.9 fusion.69
  74.9 12.2 %reduce-scatter.5.cloned.1.call-done = f32[576,768]{1,0:T(8,128)} async-done(((f32[1152,768]{1,0:T(8,128)}), f32[576,768]{1,0:T(8,128)}) %reduce-scatter.5.cloned.1.call-update) | async-done | bytes 1769488 | tf_op jit(solution)/shard_map/reduce_scatter | solution.py:192
  87.1 1.8 fusion.97
  91.8 8.2 %all-gather.9.cloned.1.call-done = bf16[1152,768]{1,0:T(8,128)(2,1)} async-done(((bf16[576,768]{1,0:T(8,128)(2,1)}), bf16[1152,768]{1,0:T(8,128)(2,1)}) %all-gather.9.cloned.1.call-update) | async-done | bytes 1769488 | tf_op jit(solution)/shard_map/all_gather | solution.py:214
  100.0 8.0 %fusion.103 = f32[1152,1536]{1,0:T(8,128)} fusion(bf16[1152,768]{1,0:T(8,128)(2,1)} %all-gather.9.cloned.1.call-done, bf16[1536,768]{1,0:T(8,128)(2,1)} %param.25), kind=kOutput, calls=%fused_computation.161 | convolution fusion | flops 2717908992 | bytes 11206656 | tf_op jit(solution)/shard_map/gd,fd->gf/dot_general | solution.py:219
  108.0 5.3 all-gather.7.cloned.1.call-done
  113.3 12.1 %convert_reduce_fusion = (f32[1536]{0:T(1024)}, bf16[1152,1536]{1,0:T(8,128)(2,1)S(1)}, f32[1152,1536]{1,0:T(8,128)}) fusion(f32[1152,1536]{1,0:T(8,128)} %fusion.103, f32[1536]{0:T(1024)S(1)} %convert_element_type.111, bf16[1152,768]{1,0:T(8,128)(2,1)} %all-gather.7.cloned.1.call-done, bf16[768,1536]{1,0:T(8,128)(2,1)S(1)} %copy-done), kind=kOutput, calls=%fused_computation.21 | convolution fusion | flops 2758605312 | bytes 21835776 | tf_op jit(solution)/shard_map/dot_general | solution.py:201
  125.4 1.8 copy-done.54
  127.2 4.7 fusion.104
  132.1 1.6 copy-done.52
  133.6 9.0 %fusion.94 = f32[1152,768]{1,0:T(8,128)} fusion(bf16[1536,768]{1,0:T(8,128)(2,1)S(1)} %copy-done.52, f32[1152,1536]{1,0:T(8,128)} %get-tuple-element.113), kind=kOutput, calls=%fused_computation.153 | convolution fusion | flops 2733834240 | bytes 12976128 | tf_op jit(solution)/shard_map/dot_general | solution.py:208
  143.4 1.7 reduce-scatter.9.cloned.1.call-done
  145.0 2.3 multiply_reduce_fusion.1
  147.3 13.4 %reduce-scatter.7.cloned.1.call-done = f32[576,768]{1,0:T(8,128)} async-done(((f32[1152,768]{1,0:T(8,128)}), f32[576,768]{1,0:T(8,128)}) %reduce-scatter.7.cloned.1.call-update) | async-done | bytes 1769488 | tf_op jit(solution)/shard_map/reduce_scatter | solution.py:207
  160.7 4.9 fusion.96
  165.9 11.3 %all-gather.11.cloned.1.call-done = bf16[1152,768]{1,0:T(8,128)(2,1)} async-done(((bf16[576,768]{1,0:T(8,128)(2,1)}), bf16[1152,768]{1,0:T(8,128)(2,1)}) %all-gather.11.cloned.1.call-update) | async-done | bytes 1769488 | tf_op jit(solution)/shard_map/all_gather | solution.py:233
  177.2 2.4 convolution_convert_fusion
  183.0 6.3 fusion.13
  191.6 10.7 %fusion.2 = f32[6,64,896]{2,1,0:T(8,128)} fusion(bf16[896,6,64]{0,2,1:T(8,128)(2,1)S(1)} %bitcast.169, f32[6,896,896]{1,2,0:T(8,128)} %get-tuple-element.112, f32[6,896]{1,0:T(8,128)S(1)} %log_add_fusion), kind=kOutput, calls=%fused_computation.10 | convolution fusion | flops 626196480 | bytes 21353472 | tf_op jit(solution)/shard_map/hqk,qha->kha/dot_general | solution.py:113
  202.3 12.1 %multiply_reduce_fusion = (f32[6,896]{1,0:T(8,128)S(1)}, f32[6,896,896]{1,2,0:T(8,128)}) fusion(f32[6,896,896]{1,2,0:T(8,128)} %get-tuple-element.112, f32[6,896]{1,0:T(8,128)S(1)} %log_add_fusion, bf16[896,6,64]{0,2,1:T(8,128)(2,1)S(1)} %bitcast.170, bf16[896,6,64]{0,2,1:T(8,128)(2,1)S(1)} %bitcast.174), kind=kOutput, calls=%fused_computation.1 | convolution fusion | flops 631008000 | bytes 39954432 | tf_op jit(solution)/shard_map/qha,kha->hqk/dot_general | solution.py:102
  214.5 13.3 %multiply_convert_fusion = bf16[6,896,896]{1,2,0:T(8,128)(2,1)S(1)} fusion(f32[6,896,896]{1,2,0:T(8,128)} %get-tuple-element.119, f32[6,896,896]{1,2,0:T(8,128)} %get-tuple-element.112, f32[6,896]{1,0:T(8,128)S(1)} %get-tuple-element.118, f32[6,896]{1,0:T(8,128)S(1)} %log_add_fusion), kind=kLoop, calls=%fused_computation | loop fusion | flops 19267584 | bytes 48211968 | tf_op jit(solution)/shard_map/convert_element_type | solution.py:104
  227.8 2.5 fusion.53
  230.3 4.2 fusion.105
  235.7 4.0 fusion.50
  240.8 5.5 fusion.15
  251.8 2.8 fusion.54
  256.4 6.1 convolution_bitcast_fusion
  262.8 8.6 %fusion.106 = f32[768,1536]{1,0:T(8,128)} fusion(bf16[1152,768]{1,0:T(8,128)(2,1)} %all-gather.7.cloned.1.call-done, bf16[1152,1536]{1,0:T(8,128)(2,1)} %copy-done.54), kind=kOutput, calls=%fused_computation.164 | convolution fusion | flops 2717908992 | bytes 10027008 | tf_op jit(solution)/shard_map/gd,gf->df/dot_general | solution.py:222
  271.4 9.8 %fusion.93 = f32[1536,768]{1,0:T(8,128)} fusion(bf16[1152,768]{1,0:T(8,128)(2,1)S(1)} %copy-done.20, f32[1152,1536]{1,0:T(8,128)} %get-tuple-element.113), kind=kOutput, calls=%fused_computation.152 | convolution fusion | flops 2733834240 | bytes 13565952 | tf_op jit(solution)/shard_map/gf,gd->fd/dot_general | solution.py:216
  281.3 1.9 fusion.68
  283.3 4.3 convolution_bitcast_fusion.1
  287.6 1.8 convert_reduce_fusion.1
  289.5 1.8 convert_reduce_fusion.2
  291.3 2.0 maximum_maximum_fusion
  293.7 82.0 %all-reduce.1 = (f32[2,384]{1,0:T(2,128)}, f32[768]{0:T(1024)}, f32[1536]{0:T(1024)}, f32[768]{0:T(1024)}) all-reduce(f32[2,384]{1,0:T(2,128)S(1)} %convert_reduce_fusion.3, f32[768]{0:T(1024)S(1)} %convert_reduce_fusion.2, f32[1536]{0:T(1024)S(1)} %copy-done.45, ...), channel_id=1, replica_groups=mesh['dp'=16,'tensor'=2] {'dp'}, use_global_device_ids=true, to_apply=%region_27.28 | all-reduce | flops 3840 | bytes 30720 | tf_op jit(solution)/shard_map/psum | solution.py:269
  375.7 2.8 fusion.38
  378.5 40.2 %all-reduce = (f32[768]{0:T(1024)}, f32[768]{0:T(1024)}, f32[768]{0:T(1024)}, f32[768]{0:T(1024)}) all-reduce(f32[768]{0:T(1024)S(1)} %get-tuple-element.72, f32[768]{0:T(1024)S(1)} %get-tuple-element.77, f32[768]{0:T(1024)S(1)} %get-tuple-element.70, f32[768]{0:T(1024)S(1)} %get-tuple-element.76), channel_id=1, replica_groups=mesh['dp'=16,'tensor'=2] {'dp','tensor'}, use_global_device_ids=true, to_apply=%region_22.23 | all-reduce | flops 3072 | bytes 24576 | tf_op jit(solution)/shard_map/psum | solution.py:266
  418.7 3.5 fusion.37
  422.2 260.7 %all-reduce.5.cloned.1.call-done = (f32[3,768,384]{1,2,0:T(8,128)}, f32[384,768]{1,0:T(8,128)}, f32[768,1536]{1,0:T(8,128)}, f32[1536,768]{1,0:T(8,128)}) async-done(((f32[3,768,384]{1,2,0:T(8,128)}, f32[384,768]{1,0:T(8,128)}, f32[768,1536]{1,0:T(8,128)}, f32[1536,768]{1,0:T(8,128)}), (f32[3,768,384]{1,2,0:T(8,128)}, f32[384,768]{1,0:T(8,128)}, f32[768,1536]{1,0:T(8,128)}, ...) | async-done | bytes 14155792 | tf_op jit(solution)/shard_map/psum | solution.py:269
  682.9 5.2 copy.191
  689.2 5.5 copy.264
  694.7 2.2 copy.265
  (199 shorter events, 38.7 us)
Async XLA Ops:
  7.2 106.1 %copy-start = (bf16[768,1536]{1,0:T(8,128)(2,1)S(1)}, bf16[768,1536]{1,0:T(8,128)(2,1)}, u32[]{:S(2)}) copy-start(bf16[768,1536]{1,0:T(8,128)(2,1)} %param.23) | copy-start | bytes 7077892
  7.2 8.3 %copy-start.46 = (bf16[2,384]{1,0:T(2,128)(2,1)S(1)}, bf16[2,384]{1,0:T(2,128)(2,1)}, u32[]{:S(2)}) copy-start(bf16[2,384]{1,0:T(2,128)(2,1)} %param.18) | copy-start | bytes 4612
  7.2 20.0 %all-gather.5.cloned.1.call-start = ((), (), s32[]{:S(2)}) async-start(), calls=%async_computation.4 | async-start | bytes 2654208 | tf_op jit(solution)/shard_map/all_gather | solution.py:181
  8.1 23.6 %copy-start.41 = (f32[768]{0:T(1024)}, f32[768]{0:T(1024)S(1)}, u32[]{:S(2)}) copy-start(f32[768]{0:T(1024)S(1)} %convert_element_type.99) | copy-start | bytes 9220
  10.2 21.6 %copy-start.39 = (f32[576]{0:T(1024)}, f32[576]{0:T(1024)S(1)}, u32[]{:S(2)}) copy-start(f32[576]{0:T(1024)S(1)} %broadcast_multiply_fusion.5) | copy-start | bytes 6916
  11.7 20.0 %copy-start.43 = (f32[576]{0:T(1024)}, f32[576]{0:T(1024)S(1)}, u32[]{:S(2)}) copy-start(f32[576]{0:T(1024)S(1)} %add_rsqrt_fusion.1) | copy-start | bytes 6916
  14.2 72.8 %reduce-scatter.5.cloned.1.call-start = ((), (), s32[]{:S(2)}) async-start(), calls=%async_computation.5 | async-start | bytes 5308416 | tf_op jit(solution)/shard_map/reduce_scatter | solution.py:192
  33.7 8.4 %copy-start.7 = (bf16[896,1,384]{0,2,1:T(8,128)(2,1)}, bf16[896,1,384]{0,2,1:T(8,128)(2,1)S(1)}, u32[]{:S(2)}) copy-start(bf16[896,1,384]{0,2,1:T(8,128)(2,1)S(1)} %get-tuple-element.99) | copy-start | bytes 2064388
  37.2 2.4 copy-start.2
  37.2 2.4 copy-start.14
  37.6 3.3 copy-start.9
  51.1 9.1 %copy-start.15 = (bf16[896,1,384]{0,2,1:T(8,128)(2,1)S(1)}, bf16[896,1,384]{0,2,1:T(8,128)(2,1)}, u32[]{:S(2)}) copy-start(bf16[896,1,384]{0,2,1:T(8,128)(2,1)} %get-tuple-element.100) | copy-start | bytes 2064388
  60.2 10.9 %copy-start.26 = (bf16[48,8,2,128]{3,1,2,0:T(8,128)(2,1)S(1)}, bf16[48,8,2,128]{3,1,2,0:T(8,128)(2,1)}, u32[]{:S(2)}) copy-start(bf16[48,8,2,128]{3,1,2,0:T(8,128)(2,1)} %copy.258) | copy-start | bytes 589828
  60.2 10.9 %copy-start.37 = (bf16[384,768]{1,0:T(8,128)(2,1)S(1)}, bf16[384,768]{1,0:T(8,128)(2,1)}, u32[]{:S(2)}) copy-start(bf16[384,768]{1,0:T(8,128)(2,1)} %param.19) | copy-start | bytes 1769476
  74.0 13.1 %copy-start.5 = (bf16[576,768]{1,0:T(8,128)(2,1)S(1)}, bf16[576,768]{1,0:T(8,128)(2,1)}, u32[]{:S(2)}) copy-start(bf16[576,768]{1,0:T(8,128)(2,1)} %param.14) | copy-start | bytes 2654212
  74.0 26.0 %all-gather.9.cloned.1.call-start = ((), (), s32[]{:S(2)}) async-start(), calls=%async_computation.8 | async-start | bytes 2654208 | tf_op jit(solution)/shard_map/all_gather | solution.py:214
  74.8 38.5 %all-gather.7.cloned.1.call-start = ((), (), s32[]{:S(2)}) async-start(), calls=%async_computation.6 | async-start | bytes 2654208 | tf_op jit(solution)/shard_map/all_gather | solution.py:200
  88.9 2.9 copy-start.47
  91.3 53.7 %reduce-scatter.9.cloned.1.call-start = ((), (), s32[]{:S(2)}) async-start(), calls=%async_computation.9 | async-start | bytes 5308416 | tf_op jit(solution)/shard_map/reduce_scatter | solution.py:224
  132.0 28.7 %reduce-scatter.7.cloned.1.call-start = ((), (), s32[]{:S(2)}) async-start(), calls=%async_computation.7 | async-start | bytes 5308416 | tf_op jit(solution)/shard_map/reduce_scatter | solution.py:207
  142.7 2.4 copy-start.4
  142.7 34.5 %all-gather.11.cloned.1.call-start = ((), (), s32[]{:S(2)}) async-start(), calls=%async_computation.10 | async-start | bytes 2654208 | tf_op jit(solution)/shard_map/all_gather | solution.py:233
  160.7 16.4 %copy-start.38 = (bf16[384,768]{1,0:T(8,128)(2,1)S(1)}, bf16[384,768]{1,0:T(8,128)(2,1)}, u32[]{:S(2)}) copy-start(bf16[384,768]{1,0:T(8,128)(2,1)} %param.19) | copy-start | bytes 1769476
  165.7 210.0 %reduce-scatter.11.cloned.1.call-start = ((), (), s32[]{:S(2)}) async-start(), calls=%async_computation.11 | async-start | bytes 5308416 | tf_op jit(solution)/shard_map/reduce_scatter | solution.py:255
  165.9 15.5 %copy-start.10 = (f32[2,6,128,128]{2,3,1,0:T(8,128)S(1)}, f32[2,6,128,128]{2,3,1,0:T(8,128)}, u32[]{:S(2)}) copy-start(f32[2,6,128,128]{2,3,1,0:T(8,128)} %copy-done.9) | copy-start | bytes 2359300
  179.6 3.4 copy-start.16
  183.0 7.6 %copy-start.25 = (bf16[2,128,6,64]{1,0,3,2:T(2,128)(2,1)S(1)}, bf16[2,128,6,64]{1,0,3,2:T(2,128)(2,1)}, u32[]{:S(2)}) copy-start(bf16[2,128,6,64]{1,0,3,2:T(2,128)(2,1)} %reshape.178) | copy-start | bytes 589828
  214.5 13.3 %copy-start.8 = (bf16[896,1,384]{0,2,1:T(8,128)(2,1)S(1)}, bf16[896,1,384]{0,2,1:T(8,128)(2,1)}, u32[]{:S(2)}) copy-start(bf16[896,1,384]{0,2,1:T(8,128)(2,1)} %copy-done.7) | copy-start | bytes 2064388
  227.8 2.5 copy-start.13
  240.8 7.0 copy-start.22
  247.9 3.9 copy-start.17
  251.8 4.6 copy-start.29
  262.5 420.4 %all-reduce.5.cloned.1.call-start = ((), (), s32[]{:S(2)}) async-start(), calls=%async_computation.12 | async-start | bytes 28311552 | tf_op jit(solution)/shard_map/psum | solution.py:269
  262.8 8.6 %copy-start.20 = (bf16[1152,768]{1,0:T(8,128)(2,1)S(1)}, bf16[1152,768]{1,0:T(8,128)(2,1)}, u32[]{:S(2)}) copy-start(bf16[1152,768]{1,0:T(8,128)(2,1)} %all-gather.9.cloned.1.call-done) | copy-start | bytes 5308420
  271.4 9.8 %copy-start.21 = (bf16[1152,768]{1,0:T(8,128)(2,1)S(1)}, bf16[1152,768]{1,0:T(8,128)(2,1)}, u32[]{:S(2)}) copy-start(bf16[1152,768]{1,0:T(8,128)(2,1)} %all-gather.11.cloned.1.call-done) | copy-start | bytes 5308420
  271.4 9.8 %copy-start.27 = (bf16[48,8,2,128]{3,1,2,0:T(8,128)(2,1)S(1)}, bf16[48,8,2,128]{3,1,2,0:T(8,128)(2,1)}, u32[]{:S(2)}) copy-start(bf16[48,8,2,128]{3,1,2,0:T(8,128)(2,1)} %copy.258) | copy-start | bytes 589828
  271.4 9.8 %copy-start.36 = (bf16[6,64,896]{2,1,0:T(8,128)(2,1)S(1)}, bf16[6,64,896]{2,1,0:T(8,128)(2,1)}, u32[]{:S(2)}) copy-start(bf16[6,64,896]{2,1,0:T(8,128)(2,1)} %copy-done.35) | copy-start | bytes 2064388
  287.6 3.7 copy-start.32
  287.6 3.6 copy-start.34
  291.3 2.4 copy-start.45
  291.3 84.4 %copy-start.40 = (f32[576]{0:T(1024)S(1)}, f32[576]{0:T(1024)}, u32[]{:S(2)}) copy-start(f32[576]{0:T(1024)} %copy-done.39) | copy-start | bytes 6916
  291.3 84.4 %copy-start.42 = (f32[768]{0:T(1024)S(1)}, f32[768]{0:T(1024)}, u32[]{:S(2)}) copy-start(f32[768]{0:T(1024)} %copy-done.41) | copy-start | bytes 9220
  291.3 84.4 %copy-start.44 = (f32[576]{0:T(1024)S(1)}, f32[576]{0:T(1024)}, u32[]{:S(2)}) copy-start(f32[576]{0:T(1024)} %copy-done.43) | copy-start | bytes 6916
  375.7 43.0 %copy-start.11 = (f32[576,768]{1,0:T(8,128)S(1)}, f32[576,768]{1,0:T(8,128)}, u32[]{:S(2)}) copy-start(f32[576,768]{1,0:T(8,128)} %reduce-scatter.11.cloned.1.call-done) | copy-start | bytes 5308420
  682.9 5.3 copy-start.23
  688.1 6.5 slice-start
  689.2 5.5 slice-start.1
  689.2 7.7 %copy-start.1 = (bf16[768,1536]{1,0:T(8,128)(2,1)S(1)}, bf16[768,1536]{1,0:T(8,128)(2,1)}, u32[]{:S(2)}) copy-start(bf16[768,1536]{1,0:T(8,128)(2,1)} %param.23) | copy-start | bytes 7077892
  (18 other events, 24.9 us)
Sparse Core Ops, SparseCore 0:
  14.4 12.8 all-gather.4
  74.2 12.8 reduce-scatter.4
  88.6 11.3 all-gather.8
  102.0 11.2 all-gather.6
  132.1 12.8 reduce-scatter.8
  147.7 12.9 reduce-scatter.6
  165.8 11.3 all-gather.10
  262.6 12.8 reduce-scatter.10
  287.7 395.0 all-reduce.4
where the time goes:
time: 711 us; the launch traced here: 704 us
  waiting for transfers between devices  325 us (46%)
  matrix products  143 us (20%)
  blocking collectives  122 us (17%)
  other arithmetic  60.1 us (8%)
  local copies, waits for them, and re-layouts  37 us (5%)
  between operations  15.1 us (2%)
    psum x1, waiting for transfers between devices, on_device(): lax.psum((grad_qkv_weight, grad_qv_bias, grad_out_weight, grad_out_bias,...  261 us
    psum x1, blocking collectives, on_device(): lax.psum((grad_qkv_weight, grad_qv_bias, grad_out_weight, grad_out_bias,...  82 us
    psum x1, blocking collectives, on_device(): lax.psum((part_ln1_gain, part_ln1_bias, part_ln2_gain, part_ln2_bias), ('...  40.2 us
    unnamed x119, local copies, waits for them, and re-layouts  23.1 us
  transfers between devices with their start and end apart: 9, of which 8 were waited for; matrix products, arithmetic and copies ran while one was open for 9% of the time, Pallas kernels for 0%

commit v1 on v0

--- a/solution.py
+++ b/solution.py
@@ -1,6 +1,10 @@
+import functools
 import jax
 import jax.numpy as jnp
 from jax import lax
+from jax.experimental import pallas as pl
+from jax.experimental.pallas import tpu as pltpu
+
 from jax.sharding import PartitionSpec as P
 
 HD = 64
@@ -152,6 +156,240 @@
     grad_key = jnp.concatenate([dk_head, dk_tail.reshape(tail_rows, heads_local, HD)], axis=0)
     grad_value = jnp.concatenate([dv_head, dv_tail.reshape(tail_rows, heads_local, HD)], axis=0)
     return (grad_query, grad_key, grad_value)
+
+
+MESH = pl.DeviceIdType.MESH
+ITEM = 1536
+SMALL = 56
+LN_ROWS = 24
+
+
+class Sum:
+    def __init__(self, part, res, rx1, rx2, rx3, ssem, rsem):
+        self.part, self.res, self.rx1, self.rx2, self.rx3 = part, res, rx1, rx2, rx3
+        self.ssem, self.rsem = ssem, rsem
+        dp, t = lax.axis_index("dp"), lax.axis_index("tensor")
+        x, y, z = lax.rem(dp, 2), lax.rem(lax.div(dp, 2), 2), lax.rem(lax.div(dp, 4), 4)
+        self.t, self.z = t, z
+        self.a = x * (1 - t) + y * t
+        self.b = y * (1 - t) + x * t
+        self.to_a = (dp + (1 + t) * (1 - 2 * self.a), t)
+        self.to_b = (dp + (2 - t) * (1 - 2 * self.b), t)
+        self.to_z = []
+        self.zs = []
+        for d in (1, 2, 3):
+            zj = lax.rem(z + d, 4)
+            self.zs.append(zj)
+            self.to_z.append((dp + 4 * (zj - z), t))
+        self.to_x = (dp + 1 - 2 * x, t)
+        self.to_y = (dp + 2 - 4 * y, t)
+        self.to_c = (dp, 1 - t)
+
+    def barrier(self):
+        bar = pltpu.get_barrier_semaphore()
+        peers = [self.to_x, self.to_y, self.to_c] + self.to_z
+        for peer in peers:
+            pl.semaphore_signal(bar, inc=1, device_id=peer, device_id_type=MESH)
+        pl.semaphore_wait(bar, len(peers))
+
+    def rows(self, offset, count):
+        return pl.ds(pl.multiple_of(offset, 32), count)
+
+    def copy(self, src, dst, k, i, peer):
+        return pltpu.make_async_remote_copy(
+            src_ref=src, dst_ref=dst, send_sem=self.ssem.at[k, i], recv_sem=self.rsem.at[k, i],
+            device_id=peer, device_id_type=MESH)
+
+    def copies(self, stage, i):
+        base = i * ITEM
+        half = base + self.a * (ITEM // 2)
+        quarter = half + self.b * (ITEM // 4)
+        block = quarter + self.z * (ITEM // 16)
+        if stage == 1:
+            src = self.part.at[self.rows(base + (1 - self.a) * (ITEM // 2), ITEM // 2)]
+            return [self.copy(src, self.rx1.at[self.rows(i * (ITEM // 2), ITEM // 2)], 0, i, self.to_a)]
+        if stage == 2:
+            src = self.part.at[self.rows(half + (1 - self.b) * (ITEM // 4), ITEM // 4)]
+            return [self.copy(src, self.rx2.at[self.rows(i * (ITEM // 4), ITEM // 4)], 1, i, self.to_b)]
+        if stage == 3:
+            out = []
+            for d in range(3):
+                src = self.part.at[self.rows(quarter + self.zs[d] * (ITEM // 16), ITEM // 16)]
+                dst = self.rx3.at[self.rows((i * 3 + d) * (ITEM // 16), ITEM // 16)]
+                out.append(self.copy(src, dst, 2 + d, i, self.to_z[d]))
+            return out
+        if stage == 4:
+            ref = self.res.at[self.rows(block, ITEM // 16)]
+            return [self.copy(ref, ref, 5 + d, i, self.to_z[d]) for d in range(3)]
+        if stage == 5:
+            ref = self.res.at[self.rows(quarter, ITEM // 4)]
+            return [self.copy(ref, ref, 8, i, self.to_b)]
+        ref = self.res.at[self.rows(half, ITEM // 2)]
+        return [self.copy(ref, ref, 9, i, self.to_a)]
+
+    def start(self, stage, i):
+        for c in self.copies(stage, i):
+            c.start()
+
+    def arrive(self, stage, i):
+        for c in self.copies(stage, i):
+            c.wait_recv()
+        half = i * ITEM + self.a * (ITEM // 2)
+        quarter = half + self.b * (ITEM // 4)
+        block = quarter + self.z * (ITEM // 16)
+        f32 = jnp.float32
+        if stage == 1:
+            own = self.rows(half, ITEM // 2)
+            got = self.rx1[self.rows(i * (ITEM // 2), ITEM // 2), :]
+            self.part[own, :] = (self.part[own, :].astype(f32) + got.astype(f32)).astype(jnp.bfloat16)
+        elif stage == 2:
+            own = self.rows(quarter, ITEM // 4)
+            got = self.rx2[self.rows(i * (ITEM // 4), ITEM // 4), :]
+            self.part[own, :] = (self.part[own, :].astype(f32) + got.astype(f32)).astype(jnp.bfloat16)
+        elif stage == 3:
+            own = self.rows(block, ITEM // 16)
+            total = self.part[own, :].astype(f32)
+            for d in range(3):
+                total = total + self.rx3[self.rows((i * 3 + d) * (ITEM // 16), ITEM // 16), :].astype(f32)
+            self.res[own, :] = total.astype(jnp.bfloat16)
+        if stage < 6:
+            self.start(stage + 1, i)
+
+    def sent(self, i):
+        for stage in range(1, 7):
+            for c in self.copies(stage, i):
+                c.wait_send()
+
+
+def small_sum(comm, small, out, land_c, land_x, land_y, land_z, acc, ssem, rsem):
+    def copy(src, dst, k, peer):
+        return pltpu.make_async_remote_copy(
+            src_ref=src, dst_ref=dst, send_sem=ssem.at[k], recv_sem=rsem.at[k],
+            device_id=peer, device_id_type=MESH)
+
+    c = copy(small.at[pl.ds(0, LN_ROWS)], land_c, 0, comm.to_c)
+    c.start()
+    yield
+    c.wait_recv()
+    acc[0] = small[...]
+    acc[0, pl.ds(0, LN_ROWS), :] = small[pl.ds(0, LN_ROWS), :] + land_c[...]
+    cx = copy(acc.at[0], land_x, 1, comm.to_x)
+    cx.start()
+    yield
+    cx.wait_recv()
+    acc[1] = acc[0] + land_x[...]
+    cy = copy(acc.at[1], land_y, 2, comm.to_y)
+    cy.start()
+    yield
+    cy.wait_recv()
+    acc[2] = acc[1] + land_y[...]
+    cz = []
+    for d in range(3):
+        cz.append(copy(acc.at[2], land_z.at[comm.z], 3 + d, comm.to_z[d]))
+        cz[-1].start()
+    yield
+    land_z[comm.z] = acc[2]
+    for d in range(3):
+        cz[d].wait_recv()
+    out[...] = (land_z[0] + land_z[1]) + (land_z[2] + land_z[3])
+    for s in [c, cx, cy] + cz:
+        s.wait_send()
+    yield
+
+
+def sum_kernel(n, part_in, small, res, small_out, part, rx1, rx2, rx3, ssem, rsem,
+               land_c, land_x, land_y, land_z, acc, ss, sr, lsem):
+    comm = Sum(part, res, rx1, rx2, rx3, ssem, rsem)
+    load = pltpu.make_async_copy(part_in, part, lsem)
+    load.start()
+    comm.barrier()
+    load.wait()
+    sm = small_sum(comm, small, small_out, land_c, land_x, land_y, land_z, acc, ss, sr)
+    next(sm)
+    lax.fori_loop(0, n, lambda i, c: (comm.start(1, i), c)[1], 0)
+    next(sm)
+
+    def step(s, c):
+        for stage in range(1, 7):
+            i = s - (stage - 1)
+
+            @pl.when((i >= 0) & (i < n))
+            def _():
+                comm.arrive(stage, i)
+        return c
+
+    lax.fori_loop(0, n + 5, step, 0)
+    next(sm)
+    next(sm)
+    next(sm)
+    lax.fori_loop(0, n, lambda i, c: (comm.sent(i), c)[1], 0)
+
+
+def sum_call(part, small):
+    n = part.shape[0] // ITEM
+    f32, bf = jnp.float32, jnp.bfloat16
+    return pl.pallas_call(
+        functools.partial(sum_kernel, n),
+        out_shape=(jax.ShapeDtypeStruct(part.shape, bf), jax.ShapeDtypeStruct(small.shape, f32)),
+        in_specs=[pl.BlockSpec(memory_space=pl.ANY), pl.BlockSpec(memory_space=pltpu.VMEM)],
+        out_specs=(pl.BlockSpec(memory_space=pltpu.VMEM), pl.BlockSpec(memory_space=pltpu.VMEM)),
+        scratch_shapes=[
+            pltpu.VMEM(part.shape, bf),
+            pltpu.VMEM((n * ITEM // 2, 128), bf),
+            pltpu.VMEM((n * ITEM // 4, 128), bf),
+            pltpu.VMEM((n * 3 * ITEM // 16, 128), bf),
+            pltpu.SemaphoreType.DMA((10, n)),
+            pltpu.SemaphoreType.DMA((10, n)),
+            pltpu.VMEM((LN_ROWS, 128), f32),
+            pltpu.VMEM((SMALL, 128), f32),
+            pltpu.VMEM((SMALL, 128), f32),
+            pltpu.VMEM((4, SMALL, 128), f32),
+            pltpu.VMEM((3, SMALL, 128), f32),
+            pltpu.SemaphoreType.DMA((6,)),
+            pltpu.SemaphoreType.DMA((6,)),
+            pltpu.SemaphoreType.DMA,
+        ],
+        compiler_params=pltpu.CompilerParams(
+            collective_id=0, has_side_effects=True, vmem_limit_bytes=56 * 2**20),
+        name="grad_sum",
+    )(part, small)
+
+
+def swap(values):
+    return lax.ppermute(values, "tensor", [(0, 1), (1, 0)])
+
+
+def gather_pair(own):
+    rows = own.shape[0]
+    t = lax.axis_index("tensor")
+    full = jnp.zeros((2 * rows,) + own.shape[1:], own.dtype)
+    full = lax.dynamic_update_slice_in_dim(full, own, t * rows, 0)
+    return lax.dynamic_update_slice_in_dim(full, swap(own), (1 - t) * rows, 0)
+
+
+def scatter_pair(part):
+    rows = part.shape[0] // 2
+    t = lax.axis_index("tensor")
+    away = lax.dynamic_slice_in_dim(part, (1 - t) * rows, rows, 0)
+    return lax.dynamic_slice_in_dim(part, t * rows, rows, 0) + swap(away)
+
+
+def blocks(values):
+    lead, rows, cols = values.shape
+    return values.reshape(lead, rows, cols // 128, 128).transpose(0, 2, 1, 3).reshape(-1, 128)
+
+
+def unblock(stacked, lead, rows, cols):
+    stacked = stacked.reshape(lead, cols // 128, rows, 128).astype(jnp.float32)
+    return stacked.transpose(0, 2, 1, 3).reshape(lead, rows, cols)
+
+
+def over_slice(values):
+    count = lax.axis_size("dp")
+    total = values
+    for shift in range(16, count, 16):
+        total = total + lax.ppermute(values, "dp", [(i, (i + shift) % count) for i in range(count)])
+    return total
 
 
 def on_device(
@@ -178,7 +416,7 @@
     gain_two = ln2_gain.astype(jnp.float32)
     x_own = tokens.astype(jnp.float32)
     normed1, normal1, inv_std1 = norm_rows(x_own, gain_one, ln1_bias.astype(jnp.float32))
-    ln1_full = lax.all_gather(normed1.astype(jnp.bfloat16), "tensor", axis=0, tiled=True)
+    ln1_full = gather_pair(normed1.astype(jnp.bfloat16))
     projected = jnp.einsum("gd,tdj->gtj", ln1_full, qkv_weight, preferred_element_type=jnp.float32)
     bias_float = qv_bias.astype(jnp.float32)
     bias_rows = jnp.stack([bias_float[0], jnp.zeros_like(bias_float[0]), bias_float[1]])
@@ -189,29 +427,19 @@
     mixed, lse_head, lse_tail = attend_forward(queries, keys_all, values)
     mixed_low = mixed.reshape(group_rows, local_width).astype(jnp.bfloat16)
     part_rows = mixed_low
-    attn_own = lax.psum_scatter(
-        jnp.dot(part_rows, out_weight, preferred_element_type=jnp.float32),
-        "tensor",
-        scatter_dimension=0,
-        tiled=True,
-    ) + out_bias.astype(jnp.float32)
+    attn_own = scatter_pair(jnp.dot(part_rows, out_weight, preferred_element_type=jnp.float32)) + out_bias.astype(jnp.float32)
     residual = x_own + attn_own
     normed2, normal2, inv_std2 = norm_rows(residual, gain_two, ln2_bias.astype(jnp.float32))
-    ln2_full = lax.all_gather(normed2.astype(jnp.bfloat16), "tensor", axis=0, tiled=True)
+    ln2_full = gather_pair(normed2.astype(jnp.bfloat16))
     pre_act = jnp.dot(ln2_full, fc_weight, preferred_element_type=jnp.float32) + fc_bias.astype(
         jnp.float32
     )
     activation, gelu_pull = jax.vjp(lambda inner: jax.nn.gelu(inner, approximate=True), pre_act)
     act_low = activation.astype(jnp.bfloat16)
     part_rows = act_low
-    mlp_own = lax.psum_scatter(
-        jnp.dot(part_rows, proj_weight, preferred_element_type=jnp.float32),
-        "tensor",
-        scatter_dimension=0,
-        tiled=True,
-    ) + proj_bias.astype(jnp.float32)
+    mlp_own = scatter_pair(jnp.dot(part_rows, proj_weight, preferred_element_type=jnp.float32)) + proj_bias.astype(jnp.float32)
     block_output = (residual + mlp_own).astype(jnp.bfloat16)
-    cot_full = lax.all_gather(cotangent, "tensor", axis=0, tiled=True)
+    cot_full = gather_pair(cotangent)
     grad_proj_bias = jnp.sum(cot_full, axis=0, dtype=jnp.float32)
     grad_proj_weight = jnp.einsum(
         "gf,gd->fd", act_low, cot_full, preferred_element_type=jnp.float32
@@ -221,16 +449,11 @@
     grad_fc_bias = jnp.sum(grad_pre, axis=0, dtype=jnp.float32)
     grad_fc_weight = jnp.einsum("gd,gf->df", ln2_full, grad_pre, preferred_element_type=jnp.float32)
     part_rows = grad_pre
-    grad_norm2 = lax.psum_scatter(
-        jnp.einsum("gf,df->gd", part_rows, fc_weight, preferred_element_type=jnp.float32),
-        "tensor",
-        scatter_dimension=0,
-        tiled=True,
-    )
+    grad_norm2 = scatter_pair(jnp.einsum("gf,df->gd", part_rows, fc_weight, preferred_element_type=jnp.float32))
     grad_resid = cotangent.astype(jnp.float32) + norm_back(grad_norm2, normal2, inv_std2, gain_two)
     part_ln2_gain = jnp.sum(grad_norm2 * normal2, axis=0)
     part_ln2_bias = jnp.sum(grad_norm2, axis=0)
-    attn_cot_full = lax.all_gather(grad_resid.astype(jnp.bfloat16), "tensor", axis=0, tiled=True)
+    attn_cot_full = gather_pair(grad_resid.astype(jnp.bfloat16))
     grad_out_bias = jnp.sum(attn_cot_full, axis=0, dtype=jnp.float32)
     grad_out_weight = jnp.einsum(
         "gj,gd->jd", mixed_low, attn_cot_full, preferred_element_type=jnp.float32
@@ -252,45 +475,56 @@
     )
     grad_qv_bias = jnp.sum(grad_proj_all[:, 0::2], axis=0, dtype=jnp.float32)
     part_rows = grad_proj_all
-    grad_norm1 = lax.psum_scatter(
-        jnp.einsum("gtj,tdj->gd", part_rows, qkv_weight, preferred_element_type=jnp.float32),
-        "tensor",
-        scatter_dimension=0,
-        tiled=True,
-    )
+    grad_norm1 = scatter_pair(jnp.einsum("gtj,tdj->gd", part_rows, qkv_weight, preferred_element_type=jnp.float32))
     input_grad = (grad_resid + norm_back(grad_norm1, normal1, inv_std1, gain_one)).astype(
         jnp.bfloat16
     )
     part_ln1_gain = jnp.sum(grad_norm1 * normal1, axis=0)
     part_ln1_bias = jnp.sum(grad_norm1, axis=0)
-    grad_ln1_gain, grad_ln1_bias, grad_ln2_gain, grad_ln2_bias = lax.psum(
-        (part_ln1_gain, part_ln1_bias, part_ln2_gain, part_ln2_bias), ("dp", "tensor")
-    )
-    summed = lax.psum(
-        (
-            grad_qkv_weight,
-            grad_qv_bias,
-            grad_out_weight,
+    width = tokens.shape[1]
+    units = fc_weight.shape[1]
+    low = jnp.bfloat16
+    part = jnp.concatenate(
+        [
+            blocks(grad_proj_weight.astype(low).reshape(units // 256, 256, width)),
+            blocks(grad_fc_weight.astype(low)[None]),
+            blocks(grad_out_weight.astype(low)[None]),
+            blocks(grad_qkv_weight.astype(low)),
+        ],
+        axis=0,
+    )
+    small = jnp.concatenate(
+        [
+            part_ln1_gain,
+            part_ln1_bias,
+            part_ln2_gain,
+            part_ln2_bias,
+            grad_qv_bias.reshape(-1),
             grad_out_bias,
-            grad_fc_weight,
             grad_fc_bias,
-            grad_proj_weight,
             grad_proj_bias,
-        ),
-        "dp",
-    )
-    grad_qkv_weight, grad_qv_bias, grad_out_weight, grad_out_bias = (
-        summed[0],
-        summed[1],
-        summed[2],
-        summed[3],
-    )
-    grad_fc_weight, grad_fc_bias, grad_proj_weight, grad_proj_bias = (
-        summed[4],
-        summed[5],
-        summed[6],
-        summed[7],
-    )
+            jnp.zeros((SMALL * 128 - 6912,), jnp.float32),
+        ]
+    ).reshape(SMALL, 128)
+    total, small = sum_call(part, small)
+    cuts = [units * width // 128]
+    cuts.append(cuts[-1] + units * width // 128)
+    cuts.append(cuts[-1] + local_width * width // 128)
+    grad_proj_weight = unblock(total[: cuts[0]], units // 256, 256, width).reshape(units, width)
+    grad_fc_weight = unblock(total[cuts[0] : cuts[1]], 1, width, units)[0]
+    grad_out_weight = unblock(total[cuts[1] : cuts[2]], 1, local_width, width)[0]
+    grad_qkv_weight = unblock(total[cuts[2] :], 3, width, local_width)
+    small = over_slice(small)
+    if lax.axis_size("dp") > 16:
+        grad_proj_weight = over_slice(grad_proj_weight)
+        grad_fc_weight = over_slice(grad_fc_weight)
+        grad_out_weight = over_slice(grad_out_weight)
+        grad_qkv_weight = over_slice(grad_qkv_weight)
+    flat = small.reshape(-1)
+    grad_ln1_gain, grad_ln1_bias = flat[:768], flat[768:1536]
+    grad_ln2_gain, grad_ln2_bias = flat[1536:2304], flat[2304:3072]
+    grad_qv_bias = flat[3072:3840].reshape(2, local_width)
+    grad_out_bias, grad_fc_bias, grad_proj_bias = flat[3840:4608], flat[4608:6144], flat[6144:6912]
     return (
         block_output,
         input_grad,

time: 711 us -> 460 us (0.65)
  waiting for transfers between devices: 325 us -> 8.65 us
  Pallas kernels: 0 us -> 144 us
  blocking collectives: 122 us -> 0 us
  local copies, waits for them, and re-layouts: 37 us -> 91.7 us
  matrix products: 143 us -> 116 us
  other arithmetic: 60.1 us -> 86.9 us
  between operations: 15.1 us -> 1.89 us
    psum x1 -> x0, waiting for transfers between devices: 261 us -> none  [on_device(): lax.psum((grad_qkv_weight, grad_qv_bias, grad_out_weight, grad_out_bias,...]
    pallas_call x0 -> x1, Pallas kernels: none -> 144 us  [sum_call(): pl.pallas_call(functools.partial(sum_kernel, n), out_shape=(jax.ShapeDtyp...]
    psum x2 -> x0, blocking collectives: 122 us -> none  [the longest x1 82 us: on_device(): lax.psum((grad_qkv_weight, grad_qv_bias, grad_out_weight, grad_out_bias,...]
    all_gather x4 -> x0, waiting for transfers between devices: 36.4 us -> none  [the longest x1 11.6 us: on_device(): lax.all_gather(normed1.astype(jnp.bfloat16), 'tensor', axis=0, tiled=True)]
    concatenate x0 -> x1, other arithmetic: none -> 33.2 us  [on_device(): jnp.concatenate([blocks(grad_proj_weight.astype(low).reshape(units // 256...]
    reduce_scatter x4 -> x0, waiting for transfers between devices: 27.3 us -> none  [the longest x1 13.4 us: on_device(): lax.psum_scatter(jnp.dot(part_rows, proj_weight, preferred_element_type=j...]
    another operation x2 -> x10, local copies, waits for them, and re-layouts: 0.41 us -> 12.8 us  [the longest x1 3.79 us: blocks(): values.reshape(lead, rows, cols // 128, 128).transpose(0, 2, 1, 3)]
    slice x0 -> x5, local copies, waits for them, and re-layouts: none -> 10.9 us  [the longest x1 3.51 us: on_device(): total[:cuts[0]]]
  transfers between devices with their start and end apart: 9 -> 8, of which waited for: 8 -> 5; matrix products, arithmetic and copies ran while one was open for 9% -> 13% of each run, Pallas kernels for 0% -> 0%
where the time goes in v1:
time: 460 us; the launch traced here: 451 us
  Pallas kernels  144 us (31%)
  matrix products  116 us (25%)
  local copies, waits for them, and re-layouts  91.7 us (20%)
  other arithmetic  86.9 us (19%)
  waiting for transfers between devices  8.65 us (2%)
    pallas_call x1, Pallas kernels, sum_call(): pl.pallas_call(functools.partial(sum_kernel, n), out_shape=(jax.ShapeDtyp...  144 us
    concatenate x1, other arithmetic, on_device(): jnp.concatenate([blocks(grad_proj_weight.astype(low).reshape(units // 256...  33.2 us
    unnamed x147, local copies, waits for them, and re-layouts  25.7 us
    convert_element_type x1, other arithmetic, attend_back(): dscore_head = (prob_head * (dprob_head - row_dot)).astype(jnp.bfloat16)  13.5 us
    dot_general x1, matrix products, attend_back(): jnp.einsum('qha,kha->hqk', g_head, v_head, preferred_element_type=jnp.flo...  12.1 us
    dot_general x1, matrix products, attend_back(): jnp.einsum('hqk,qha->kha', prob_head.astype(jnp.bfloat16), g_head, prefer...  10.7 us
    dot_general x1, matrix products, attend_forward(): jnp.einsum('hqk,kha->qha', prob_head, v_head, preferred_element_type=jnp....  10.3 us
  transfers between devices with their start and end apart: 8, of which 5 were waited for; matrix products, arithmetic and copies ran while one was open for 13% of the time, Pallas kernels for 0%

profile of v1, /device:TPU:0, one launch (start us, length us, event | category | flops | bytes accessed | tf_op | source)
XLA Modules:
  0.0 451.3 jit_solution(11920383401424724769)
XLA Ops:
  11.1 2.2 constant_dynamic-update-slice_fusion.15
  13.3 4.5 add_convert_fusion
  23.3 2.1 bitcast_reduce_fusion
  30.7 8.8 %fusion.105 = (f32[6,896]{1,0:T(8,128)S(1)}, f32[6,896,896]{1,2,0:T(8,128)}) fusion(bf16[896,6,64]{0,2,1:T(8,128)(2,1)S(1)} %bitcast.234, bf16[896,6,64]{0,2,1:T(8,128)(2,1)S(1)} %bitcast.222, pred[896,896]{0,1:T(8,128)(4,1)S(1)} %copy-done.29), kind=kOutput, calls=%fused_computation.194 | convolution fusion | flops 631008000 | bytes 21468160 | tf_op jit(solution)/shard_map/qha,kha->hqk/dot_general | solution.py:51
  39.6 9.0 %fusion = f32[6,896]{1,0:T(8,128)S(1)} fusion(f32[6,896,896]{1,2,0:T(8,128)} %get-tuple-element.106, f32[6,896]{1,0:T(8,128)S(1)} %get-tuple-element.105), kind=kLoop, calls=%fused_computation.6 | loop fusion | flops 9628416 | bytes 19310592 | tf_op jit(solution)/shard_map/reduce_sum | solution.py:74
  48.6 10.3 %fusion.59 = bf16[6,64,896]{2,1,0:T(8,128)(2,1)S(1)} fusion(bf16[896,6,64]{0,2,1:T(8,128)(2,1)} %bitcast.238, f32[6,896,896]{1,2,0:T(8,128)} %get-tuple-element.106, f32[6,896]{1,0:T(8,128)S(1)} %fusion, f32[6,896]{1,0:T(8,128)S(1)} %get-tuple-element.105), kind=kOutput, calls=%fused_computation.94 | convolution fusion | flops 631357440 | bytes 20686848 | tf_op jit(solution)/shard_map/hqk,kha->qha/dot_general | solution.py:77
  61.6 2.4 collective-permute-done.1
  69.3 2.9 convolution_add_fusion
  72.3 4.7 %fusion.96 = f32[1152,768]{1,0:T(8,128)S(1)} fusion(bf16[1536,768]{1,0:T(8,128)(2,1)S(1)} %copy-done, f32[1152,1536]{1,0:T(8,128)S(1)} %convolution_add_fusion), kind=kOutput, calls=%fused_computation.187 | convolution fusion | flops 2733834240 | bytes 12976128 | tf_op jit(solution)/shard_map/dot_general | solution.py:440
  77.0 7.7 %convert_reduce_fusion = (f32[1536]{0:T(1024)}, bf16[1152,1536]{1,0:T(8,128)(2,1)S(1)}) fusion(f32[1152,1536]{1,0:T(8,128)S(1)} %convolution_add_fusion, bf16[1152,768]{1,0:T(8,128)(2,1)S(1)} %constant_dynamic-update-slice_fusion.11, bf16[1536,768]{1,0:T(8,128)(2,1)S(1)} %copy-done), kind=kOutput, calls=%fused_computation.22 | convolution fusion | flops 2756835840 | bytes 14751744 | tf_op jit(solution)/shard_map/gd,fd->gf/dot_general | solution.py:447
  84.7 3.0 fusion.106
  91.1 2.5 convert_reduce_fusion.1
  94.6 2.5 collective-permute-done.5
  97.2 4.9 %multiply_reduce_fusion.1 = (f32[768]{0:T(1024)S(1)}, f32[576]{0:T(1024)S(1)}, f32[576]{0:T(1024)S(1)}, f32[768]{0:T(1024)S(1)}, f32[576,768]{1,0:T(8,128)S(1)}, /*index=5*/bf16[576,768]{1,0:T(8,128)(2,1)}) fusion(f32[576,768]{1,0:T(8,128)S(1)} %copy-done.4, f32[576]{0:T(1024)S(1)} %add_rsqrt_fusion, f32[576]{0:T(1024)S(1)} %broadcast_multiply_fusion.4, ...), kind=kLoop, calls=%fused_computation.73 | loop fusion | flops 6190464 | bytes 11523076 | tf_op jit(solution)/shard_map/reduce_sum | solution.py:454
  102.2 2.2 constant_dynamic-update-slice_fusion.10
  106.0 4.2 convolution_convert_fusion.1
  110.2 3.8 reshape_reshape.9
  114.0 4.0 copy.221
  118.0 4.7 %convolution_convert_fusion = bf16[768,1536]{1,0:T(8,128)(2,1)} fusion(bf16[1152,768]{1,0:T(8,128)(2,1)S(1)} %copy-done.33, bf16[1152,1536]{1,0:T(8,128)(2,1)S(1)} %copy-done.63), kind=kOutput, calls=%fused_computation.43 | convolution fusion | flops 2719088640 | bytes 7667712 | tf_op jit(solution)/shard_map/gd,gf->df/dot_general | solution.py:450
  122.7 2.8 copy.222
  125.5 2.4 copy.223
  128.0 2.2 constant_dynamic-update-slice_fusion.9
  130.1 3.6 convolution_convert_fusion.3
  138.5 6.3 %fusion.13 = (f32[2,6,128]{2,0,1:T(2,128)S(1)}, f32[6,896,2,128]{3,1,2,0:T(8,128)}) fusion(f32[6,896,2,128]{3,1,2,0:T(8,128)} %copy-done.2, f32[2,6,128]{2,0,1:T(2,128)S(1)} %get-tuple-element.74, bf16[896,6,64,1]{0,2,3,1:T(8,128)(2,1)S(1)} %bitcast.240, bf16[2,128,6,64]{1,0,3,2:T(2,128)(2,1)S(1)} %reshape.256), kind=kOutput, calls=%fused_computation.26 | convolution fusion | flops 181664256 | bytes 11907072 | tf_op jit(solution)/shard_map/ncha,kha->nhck/dot_general | solution.py:123
  147.0 10.7 %fusion.2 = f32[6,64,896]{2,1,0:T(8,128)} fusion(bf16[896,6,64]{0,2,1:T(8,128)(2,1)S(1)} %bitcast.236, f32[6,896,896]{1,2,0:T(8,128)} %get-tuple-element.106, f32[6,896]{1,0:T(8,128)S(1)} %log_add_fusion), kind=kOutput, calls=%fused_computation.10 | convolution fusion | flops 626196480 | bytes 21353472 | tf_op jit(solution)/shard_map/hqk,qha->kha/dot_general | solution.py:117
  157.7 12.1 %multiply_reduce_fusion = (f32[6,896]{1,0:T(8,128)S(1)}, f32[6,896,896]{1,2,0:T(8,128)}) fusion(f32[6,896,896]{1,2,0:T(8,128)} %get-tuple-element.106, f32[6,896]{1,0:T(8,128)S(1)} %log_add_fusion, bf16[896,6,64]{0,2,1:T(8,128)(2,1)S(1)} %bitcast.237, bf16[896,6,64]{0,2,1:T(8,128)(2,1)S(1)} %bitcast.241), kind=kOutput, calls=%fused_computation.1 | convolution fusion | flops 631008000 | bytes 39954432 | tf_op jit(solution)/shard_map/qha,kha->hqk/dot_general | solution.py:106
  169.8 13.5 %multiply_convert_fusion = bf16[6,896,896]{1,2,0:T(8,128)(2,1)S(1)} fusion(f32[6,896,896]{1,2,0:T(8,128)} %get-tuple-element.112, f32[6,896,896]{1,2,0:T(8,128)} %get-tuple-element.106, f32[6,896]{1,0:T(8,128)S(1)} %get-tuple-element.111, f32[6,896]{1,0:T(8,128)S(1)} %log_add_fusion), kind=kLoop, calls=%fused_computation | loop fusion | flops 19267584 | bytes 48211968 | tf_op jit(solution)/shard_map/convert_element_type | solution.py:108
  183.4 2.5 fusion.57
  185.9 4.2 fusion.107
  191.2 4.0 fusion.54
  196.4 5.5 %fusion.15 = bf16[2,6,128,896]{2,3,0,1:T(8,128)(2,1)S(1)} fusion(f32[6,896,2,128]{3,1,2,0:T(8,128)} %get-tuple-element.108, f32[6,896,2,128]{3,1,2,0:T(8,128)} %copy-done.2, f32[2,6,128]{2,0,1:T(2,128)S(1)} %copy_add_fusion, f32[2,6,128]{2,0,1:T(2,128)S(1)} %get-tuple-element.74), kind=kLoop, calls=%fused_computation.28 | loop fusion | flops 6881280 | bytes 13774848 | tf_op jit(solution)/shard_map/convert_element_type | solution.py:128
  207.2 2.8 fusion.58
  211.9 2.1 maximum_maximum_fusion
  214.0 4.2 fusion.43
  218.4 4.3 convolution_bitcast_fusion
  225.2 2.2 copy.227
  229.7 33.2 %pad_maximum_fusion.part_in = bf16[27648,128]{1,0:T(8,128)(2,1)} fusion(bf16[6912,128]{1,0:T(8,128)(2,1)} %bitcast.232, bf16[2304,128]{1,0:T(8,128)(2,1)S(1)} %bitcast.247, bf16[9216,128]{1,0:T(8,128)(2,1)S(1)} %bitcast.227, bf16[9216,128]{1,0:T(8,128)(2,1)} %bitcast.228), kind=kLoop, calls=%fused_computation.21 | loop fusion | flops 28311552 | bytes 14155776 | tf_op jit(solution)/shard_map/concatenate | solution.py:487
  262.9 2.0 fusion.38
  265.7 143.8 %grad_sum.1 = (bf16[27648,128]{1,0:T(8,128)(2,1)}, f32[56,128]{1,0:T(8,128)}) custom-call(bf16[27648,128]{1,0:T(8,128)(2,1)} %pad_maximum_fusion.part_in, f32[56,128]{1,0:T(8,128)} %bitcast.256), custom_call_target="tpu_custom_call" | custom-call | tf_op jit(solution)/shard_map/grad_sum/pallas_call | solution.py:331
  414.1 2.8 slice.141
  416.9 3.5 fusion.100
  421.0 2.3 copy.229
  423.3 2.7 copy.233
  425.9 4.0 copy.228
  430.0 5.2 %copy.232 = f32[3,768,384]{2,1,0:T(8,128)} copy(f32[3,768,384]{1,2,0:T(8,128)} %bitcast.225) | data formatting | bytes 7077888
  435.1 3.1 copy.230
  438.3 6.2 %copy.234 = f32[768,1536]{1,0:T(8,128)} copy(f32[768,1536]{0,1:T(8,128)} %bitcast.220) | data formatting | bytes 9437184
  445.9 3.4 copy.303
  (249 shorter events, 65.7 us)
Async XLA Ops:
  0.6 71.6 %copy-start = (bf16[1536,768]{1,0:T(8,128)(2,1)S(1)}, bf16[1536,768]{1,0:T(8,128)(2,1)}, u32[]{:S(2)}) copy-start(bf16[1536,768]{1,0:T(8,128)(2,1)} %param.25) | copy-start | bytes 7077892
  0.7 5.9 %copy-start.5 = (bf16[576,768]{1,0:T(8,128)(2,1)S(1)}, bf16[576,768]{1,0:T(8,128)(2,1)}, u32[]{:S(2)}) copy-start(bf16[576,768]{1,0:T(8,128)(2,1)} %param.14) | copy-start | bytes 2654212
  1.5 6.7 %copy-start.46 = (f32[768]{0:T(1024)}, f32[768]{0:T(1024)S(1)}, u32[]{:S(2)}) copy-start(f32[768]{0:T(1024)S(1)} %convert_element_type.146) | copy-start | bytes 9220
  3.7 4.6 %copy-start.44 = (f32[576]{0:T(1024)}, f32[576]{0:T(1024)S(1)}, u32[]{:S(2)}) copy-start(f32[576]{0:T(1024)S(1)} %broadcast_multiply_fusion.5) | copy-start | bytes 6916
  5.2 4.7 %copy-start.54 = (bf16[2,384]{1,0:T(2,128)(2,1)S(1)}, bf16[2,384]{1,0:T(2,128)(2,1)}, u32[]{:S(2)}) copy-start(bf16[2,384]{1,0:T(2,128)(2,1)} %param.18) | copy-start | bytes 4612
  5.3 8.0 %copy-start.48 = (f32[576]{0:T(1024)}, f32[576]{0:T(1024)S(1)}, u32[]{:S(2)}) copy-start(f32[576]{0:T(1024)S(1)} %add_rsqrt_fusion.1) | copy-start | bytes 6916
  8.2 2.9 collective-permute-start
  25.4 2.4 copy-start.2
  25.8 3.3 copy-start.9
  48.6 10.3 %copy-start.38 = (bf16[48,8,2,128]{3,1,2,0:T(8,128)(2,1)S(1)}, bf16[48,8,2,128]{3,1,2,0:T(8,128)(2,1)}, u32[]{:S(2)}) copy-start(bf16[48,8,2,128]{3,1,2,0:T(8,128)(2,1)} %copy.304) | copy-start | bytes 589828
  48.6 10.3 %copy-start.42 = (bf16[384,768]{1,0:T(8,128)(2,1)S(1)}, bf16[384,768]{1,0:T(8,128)(2,1)}, u32[]{:S(2)}) copy-start(bf16[384,768]{1,0:T(8,128)(2,1)} %param.19) | copy-start | bytes 1769476
  60.2 3.8 collective-permute-start.1
  61.2 5.0 %collective-permute-start.4 = (bf16[576,768]{1,0:T(8,128)(2,1)S(1)}, bf16[576,768]{1,0:T(8,128)(2,1)S(1)}, u32[]{:S(2)}, u32[]{:S(2)}) collective-permute-start(bf16[576,768]{1,0:T(8,128)(2,1)S(1)} %copy-done.24), channel_id=1, source_target_pairs={{0,1},{1,0},{2,3},{3,2},{4,5},{5,4},{6,7},{7,6},{8,9},{9,8},{10,11... | collective-permute-start | bytes 2654216 | tf_op jit(solution)/shard_map/ppermute | solution.py:359
  65.6 2.4 collective-permute-start.2
  66.1 3.2 copy-start.60
  66.3 10.7 %copy-start.17 = (bf16[1152,768]{1,0:T(8,128)(2,1)}, bf16[1152,768]{1,0:T(8,128)(2,1)S(1)}, u32[]{:S(2)}) copy-start(bf16[1152,768]{1,0:T(8,128)(2,1)S(1)} %constant_dynamic-update-slice_fusion.11) | copy-start | bytes 5308420
  72.3 4.7 %copy-start.64 = (f32[1152,1536]{1,0:T(8,128)}, f32[1152,1536]{1,0:T(8,128)S(1)}, u32[]{:S(2)}) copy-start(f32[1152,1536]{1,0:T(8,128)S(1)} %convolution_add_fusion) | copy-start | bytes 21233668
  77.0 12.3 %copy-start.27 = (f32[1152,768]{1,0:T(8,128)}, f32[1152,768]{1,0:T(8,128)S(1)}, u32[]{:S(2)}) copy-start(f32[1152,768]{1,0:T(8,128)S(1)} %fusion.96) | copy-start | bytes 10616836
  84.7 3.0 copy-start.62
  87.7 2.9 copy-start.28
  89.2 7.9 %copy-start.4 = (f32[576,768]{1,0:T(8,128)S(1)}, f32[576,768]{1,0:T(8,128)}, u32[]{:S(2)}) copy-start(f32[576,768]{1,0:T(8,128)} %copy-done.3) | copy-start | bytes 5308420
  90.6 4.0 collective-permute-start.3
  91.0 6.2 %collective-permute-start.5 = (f32[576,768]{1,0:T(8,128)}, f32[576,768]{1,0:T(8,128)}, u32[]{:S(2)}, u32[]{:S(2)}) collective-permute-start(f32[576,768]{1,0:T(8,128)} %constant_dynamic-slice_fusion.1), channel_id=1, source_target_pairs={{0,1},{1,0},{2,3},{3,2},{4,5},{5,4},{6,7},{7,6},{8,9},{9,8},{10,11... | collective-permute-start | bytes 5308424 | tf_op jit(solution)/shard_map/ppermute | solution.py:359
  91.1 14.8 %slice-start = ((s8[7077888]{0:T(1024)(128)(4,1)}), s8[4194304]{0:T(1024)(128)(4,1)S(1)}, s32[]{:S(2)}) async-start(s8[7077888]{0:T(1024)(128)(4,1)} %bitcast.257), calls=%async_computation | async-start | bytes 8388608
  93.7 8.5 %copy-start.25 = (bf16[576,768]{1,0:T(8,128)(2,1)S(1)}, bf16[576,768]{1,0:T(8,128)(2,1)}, u32[]{:S(2)}) copy-start(bf16[576,768]{1,0:T(8,128)(2,1)} %param.27) | copy-start | bytes 2654212
  93.7 12.3 %slice-start.1 = ((s8[7077888]{0:T(1024)(128)(4,1)}), s8[2883584]{0:T(1024)(128)(4,1)S(1)}, s32[]{:S(2)}) async-start(s8[7077888]{0:T(1024)(128)(4,1)} %bitcast.257), calls=%async_computation.1 | async-start | bytes 5767168
  102.2 3.8 copy-start.18
  105.6 22.4 %collective-permute-start.6 = (bf16[576,768]{1,0:T(8,128)(2,1)}, bf16[576,768]{1,0:T(8,128)(2,1)}, u32[]{:S(2)}, u32[]{:S(2)}) collective-permute-start(bf16[576,768]{1,0:T(8,128)(2,1)} %get-tuple-element.72), channel_id=1, source_target_pairs={{0,1},{1,0},{2,3},{3,2},{4,5},{5,4},{6,7},{7,6},{8,9},{9,8},{10,11... | collective-permute-start | bytes 2654216 | tf_op jit(solution)/shard_map/ppermute | solution.py:359
  114.0 4.0 copy-start.33
  114.0 4.0 copy-start.63
  130.1 3.6 copy-start.16
  130.1 4.0 copy-start.43
  134.1 2.7 copy-start.10
  135.1 3.4 copy-start.22
  169.8 13.5 %copy-start.8 = (bf16[896,1,384]{0,2,1:T(8,128)(2,1)S(1)}, bf16[896,1,384]{0,2,1:T(8,128)(2,1)}, u32[]{:S(2)}) copy-start(bf16[896,1,384]{0,2,1:T(8,128)(2,1)} %get-tuple-element.86) | copy-start | bytes 2064388
  183.3 2.5 copy-start.20
  196.3 7.0 %copy-start.34 = (f32[2,128,6,64]{1,3,0,2:T(8,128)S(1)}, f32[2,128,6,64]{1,3,0,2:T(8,128)}, u32[]{:S(2)}) copy-start(f32[2,128,6,64]{1,3,0,2:T(8,128)} %convolution_bitcast_fusion.2) | copy-start | bytes 1179652
  203.4 3.9 copy-start.23
  207.2 4.6 %copy-start.39 = (bf16[256,1,384]{2,0,1:T(8,128)(2,1)S(1)}, bf16[256,1,384]{2,0,1:T(8,128)(2,1)}, u32[]{:S(2)}) copy-start(bf16[256,1,384]{2,0,1:T(8,128)(2,1)} %copy.220) | copy-start | bytes 589828
  213.9 4.5 copy-start.61
  229.1 33.8 %collective-permute-start.7 = (f32[576,768]{1,0:T(8,128)S(1)}, f32[576,768]{1,0:T(8,128)S(1)}, u32[]{:S(2)}, u32[]{:S(2)}) collective-permute-start(f32[576,768]{1,0:T(8,128)S(1)} %constant_dynamic-slice_fusion), channel_id=1, source_target_pairs={{0,1},{1,0},{2,3},{3,2},{4,5},{5,4},{6,7},{7,6},{8,9},{9,8},{10,11... | collective-permute-start | bytes 5308424 | tf_op jit(solution)/shard_map/ppermute | solution.py:359
  229.7 33.2 %copy-start.26 = (f32[1152,768]{1,0:T(8,128)S(1)}, f32[1152,768]{1,0:T(8,128)}, u32[]{:S(2)}) copy-start(f32[1152,768]{1,0:T(8,128)} %convolution_bitcast_fusion) | copy-start | bytes 10616836
  229.7 33.2 %copy-start.45 = (f32[576]{0:T(1024)S(1)}, f32[576]{0:T(1024)}, u32[]{:S(2)}) copy-start(f32[576]{0:T(1024)} %copy-done.44) | copy-start | bytes 6916
  229.7 33.2 %copy-start.47 = (f32[768]{0:T(1024)S(1)}, f32[768]{0:T(1024)}, u32[]{:S(2)}) copy-start(f32[768]{0:T(1024)} %copy-done.46) | copy-start | bytes 9220
  229.7 33.2 %copy-start.49 = (f32[576]{0:T(1024)S(1)}, f32[576]{0:T(1024)}, u32[]{:S(2)}) copy-start(f32[576]{0:T(1024)} %copy-done.48) | copy-start | bytes 6916
  438.3 6.2 %copy-start.12 = (bf16[9216,128]{1,0:T(8,128)(2,1)S(1)}, bf16[9216,128]{1,0:T(8,128)(2,1)}, u32[]{:S(2)}) copy-start(bf16[9216,128]{1,0:T(8,128)(2,1)} %get-tuple-element.83) | copy-start | bytes 7077892
  445.9 3.4 copy-start.13
  445.9 3.4 copy-start.14
  (27 other events, 42.9 us)

commit v2 on v1

v2 whole, which is shorter than its diff:
```python
import functools
import jax
import jax.numpy as jnp
from jax import lax
from jax.experimental import pallas as pl
from jax.experimental.pallas import tpu as pltpu

from jax.sharding import PartitionSpec as P

HD = 64
PROMPT = 896
CONT = 128
NCONT = 2


EPSILON = 1e-05
MASKED = -1e30


def norm_rows(values, gain_vec, shift_vec):
    mean_row = jnp.mean(values, axis=-1, keepdims=True)
    centred = values - mean_row
    inv_std = lax.rsqrt(jnp.mean(centred * centred, axis=-1, keepdims=True) + EPSILON)
    normal = centred * inv_std
    return (normal * gain_vec + shift_vec, normal, inv_std)


def norm_back(grad_out, normal, inv_std, gain_vec):
    scaled = grad_out * gain_vec
    inner = (
        scaled
        - jnp.mean(scaled, axis=-1, keepdims=True)
        - normal * jnp.mean(scaled * normal, axis=-1, keepdims=True)
    )
    return inner * inv_std


MESH = pl.DeviceIdType.MESH
ITEM = 1536
SMALL = 56
LN_ROWS = 24


class Sum:
    def __init__(self, part, res, rx1, rx2, rx3, ssem, rsem):
        self.part, self.res, self.rx1, self.rx2, self.rx3 = part, res, rx1, rx2, rx3
        self.ssem, self.rsem = ssem, rsem
        dp, t = lax.axis_index("dp"), lax.axis_index("tensor")
        x, y, z = lax.rem(dp, 2), lax.rem(lax.div(dp, 2), 2), lax.rem(lax.div(dp, 4), 4)
        self.t, self.z = t, z
        self.a = x * (1 - t) + y * t
        self.b = y * (1 - t) + x * t
        self.to_a = (dp + (1 + t) * (1 - 2 * self.a), t)
        self.to_b = (dp + (2 - t) * (1 - 2 * self.b), t)
        self.to_z = []
        self.zs = []
        for d in (1, 2, 3):
            zj = lax.rem(z + d, 4)
            self.zs.append(zj)
            self.to_z.append((dp + 4 * (zj - z), t))
        self.to_x = (dp + 1 - 2 * x, t)
        self.to_y = (dp + 2 - 4 * y, t)
        self.to_c = (dp, 1 - t)

    def barrier(self):
        bar = pltpu.get_barrier_semaphore()
        peers = [self.to_x, self.to_y, self.to_c] + self.to_z
        for peer in peers:
            pl.semaphore_signal(bar, inc=1, device_id=peer, device_id_type=MESH)
        pl.semaphore_wait(bar, len(peers))

    def rows(self, offset, count):
        return pl.ds(pl.multiple_of(offset, 32), count)

    def copy(self, src, dst, k, i, peer):
        return pltpu.make_async_remote_copy(
            src_ref=src, dst_ref=dst, send_sem=self.ssem.at[k, i], recv_sem=self.rsem.at[k, i],
            device_id=peer, device_id_type=MESH)

    def copies(self, stage, i):
        base = i * ITEM
        half = base + self.a * (ITEM // 2)
        quarter = half + self.b * (ITEM // 4)
        block = quarter + self.z * (ITEM // 16)
        if stage == 1:
            src = self.part.at[self.rows(base + (1 - self.a) * (ITEM // 2), ITEM // 2)]
            return [self.copy(src, self.rx1.at[self.rows(i * (ITEM // 2), ITEM // 2)], 0, i, self.to_a)]
        if stage == 2:
            src = self.part.at[self.rows(half + (1 - self.b) * (ITEM // 4), ITEM // 4)]
            return [self.copy(src, self.rx2.at[self.rows(i * (ITEM // 4), ITEM // 4)], 1, i, self.to_b)]
        if stage == 3:
            out = []
            for d in range(3):
                src = self.part.at[self.rows(quarter + self.zs[d] * (ITEM // 16), ITEM // 16)]
                dst = self.rx3.at[self.rows((i * 3 + d) * (ITEM // 16), ITEM // 16)]
                out.append(self.copy(src, dst, 2 + d, i, self.to_z[d]))
            return out
        if stage == 4:
            ref = self.res.at[self.rows(block, ITEM // 16)]
            return [self.copy(ref, ref, 5 + d, i, self.to_z[d]) for d in range(3)]
        if stage == 5:
            ref = self.res.at[self.rows(quarter, ITEM // 4)]
            return [self.copy(ref, ref, 8, i, self.to_b)]
        ref = self.res.at[self.rows(half, ITEM // 2)]
        return [self.copy(ref, ref, 9, i, self.to_a)]

    def start(self, stage, i):
        for c in self.copies(stage, i):
            c.start()

    def arrive(self, stage, i):
        for c in self.copies(stage, i):
            c.wait_recv()
        half = i * ITEM + self.a * (ITEM // 2)
        quarter = half + self.b * (ITEM // 4)
        block = quarter + self.z * (ITEM // 16)
        f32 = jnp.float32
        if stage == 1:
            own = self.rows(half, ITEM // 2)
            got = self.rx1[self.rows(i * (ITEM // 2), ITEM // 2), :]
            self.part[own, :] = (self.part[own, :].astype(f32) + got.astype(f32)).astype(jnp.bfloat16)
        elif stage == 2:
            own = self.rows(quarter, ITEM // 4)
            got = self.rx2[self.rows(i * (ITEM // 4), ITEM // 4), :]
            self.part[own, :] = (self.part[own, :].astype(f32) + got.astype(f32)).astype(jnp.bfloat16)
        elif stage == 3:
            own = self.rows(block, ITEM // 16)
            total = self.part[own, :].astype(f32)
            for d in range(3):
                total = total + self.rx3[self.rows((i * 3 + d) * (ITEM // 16), ITEM // 16), :].astype(f32)
            self.res[own, :] = total.astype(jnp.bfloat16)
        if stage < 6:
            self.start(stage + 1, i)

    def sent(self, i):
        for stage in range(1, 7):
            for c in self.copies(stage, i):
                c.wait_send()


def small_sum(comm, small, out, land_c, land_x, land_y, land_z, acc, ssem, rsem):
    def copy(src, dst, k, peer):
        return pltpu.make_async_remote_copy(
            src_ref=src, dst_ref=dst, send_sem=ssem.at[k], recv_sem=rsem.at[k],
            device_id=peer, device_id_type=MESH)

    c = copy(small.at[pl.ds(0, LN_ROWS)], land_c, 0, comm.to_c)
    c.start()
    yield
    c.wait_recv()
    acc[0] = small[...]
    acc[0, pl.ds(0, LN_ROWS), :] = small[pl.ds(0, LN_ROWS), :] + land_c[...]
    cx = copy(acc.at[0], land_x, 1, comm.to_x)
    cx.start()
    yield
    cx.wait_recv()
    acc[1] = acc[0] + land_x[...]
    cy = copy(acc.at[1], land_y, 2, comm.to_y)
    cy.start()
    yield
    cy.wait_recv()
    acc[2] = acc[1] + land_y[...]
    cz = []
    for d in range(3):
        cz.append(copy(acc.at[2], land_z.at[comm.z], 3 + d, comm.to_z[d]))
        cz[-1].start()
    yield
    land_z[comm.z] = acc[2]
    for d in range(3):
        cz[d].wait_recv()
    out[...] = (land_z[0] + land_z[1]) + (land_z[2] + land_z[3])
    for s in [c, cx, cy] + cz:
        s.wait_send()
    yield


def sum_kernel(n, *refs):
    (part_p, part_f, part_a, small, res, small_out, part, rx1, rx2, rx3, ssem, rsem,
     land_c, land_x, land_y, land_z, acc, ss, sr, lsem) = refs
    comm = Sum(part, res, rx1, rx2, rx3, ssem, rsem)
    third = n // 3 * ITEM
    loads = [
        pltpu.make_async_copy(ref, part.at[pl.ds(k * third, third)], lsem.at[k])
        for k, ref in enumerate((part_p, part_f, part_a))
    ]
    for load in loads:
        load.start()
    comm.barrier()
    for load in loads:
        load.wait()
    sm = small_sum(comm, small, small_out, land_c, land_x, land_y, land_z, acc, ss, sr)
    next(sm)
    lax.fori_loop(0, n, lambda i, c: (comm.start(1, i), c)[1], 0)
    next(sm)

    def step(s, c):
        for stage in range(1, 7):
            i = s - (stage - 1)

            @pl.when((i >= 0) & (i < n))
            def _():
                comm.arrive(stage, i)
        return c

    lax.fori_loop(0, n + 5, step, 0)
    next(sm)
    next(sm)
    next(sm)
    lax.fori_loop(0, n, lambda i, c: (comm.sent(i), c)[1], 0)


def sum_call(parts, small):
    shape = (sum(part.shape[0] for part in parts), 128)
    n = shape[0] // ITEM
    f32, bf = jnp.float32, jnp.bfloat16
    return pl.pallas_call(
        functools.partial(sum_kernel, n),
        out_shape=(jax.ShapeDtypeStruct(shape, bf), jax.ShapeDtypeStruct(small.shape, f32)),
        in_specs=[pl.BlockSpec(memory_space=pl.ANY)] * 3 + [pl.BlockSpec(memory_space=pltpu.VMEM)],
        out_specs=(pl.BlockSpec(memory_space=pltpu.VMEM), pl.BlockSpec(memory_space=pltpu.VMEM)),
        scratch_shapes=[
            pltpu.VMEM(shape, bf),
            pltpu.VMEM((n * ITEM // 2, 128), bf),
            pltpu.VMEM((n * ITEM // 4, 128), bf),
            pltpu.VMEM((n * 3 * ITEM // 16, 128), bf),
            pltpu.SemaphoreType.DMA((10, n)),
            pltpu.SemaphoreType.DMA((10, n)),
            pltpu.VMEM((LN_ROWS, 128), f32),
            pltpu.VMEM((SMALL, 128), f32),
            pltpu.VMEM((SMALL, 128), f32),
            pltpu.VMEM((4, SMALL, 128), f32),
            pltpu.VMEM((3, SMALL, 128), f32),
            pltpu.SemaphoreType.DMA((6,)),
            pltpu.SemaphoreType.DMA((6,)),
            pltpu.SemaphoreType.DMA((3,)),
        ],
        compiler_params=pltpu.CompilerParams(
            collective_id=0, has_side_effects=True, vmem_limit_bytes=56 * 2**20),
        name="grad_sum",
    )(*parts, small)


def swap(values):
    return lax.ppermute(values, "tensor", [(0, 1), (1, 0)])


def gather_pair(own):
    rows = own.shape[0]
    t = lax.axis_index("tensor")
    full = jnp.zeros((2 * rows,) + own.shape[1:], own.dtype)
    full = lax.dynamic_update_slice_in_dim(full, own, t * rows, 0)
    return lax.dynamic_update_slice_in_dim(full, swap(own), (1 - t) * rows, 0)


def scatter_pair(part):
    rows = part.shape[0] // 2
    t = lax.axis_index("tensor")
    away = lax.dynamic_slice_in_dim(part, (1 - t) * rows, rows, 0)
    return lax.dynamic_slice_in_dim(part, t * rows, rows, 0) + swap(away)


def dot(lhs, rhs, lhs_dim, rhs_dim):
    return lax.dot_general(
        lhs, rhs, (((lhs_dim,), (rhs_dim,)), ((), ())), preferred_element_type=jnp.float32)


BLOCK = 128
PROMPT_BLOCKS = PROMPT // BLOCK
GROUP = PROMPT + NCONT * CONT


def head_lanes(which):
    lane = lax.broadcasted_iota(jnp.int32, (1, 128), 1)
    return (lane >= which * HD) & (lane < (which + 1) * HD)


def own_mask():
    row_pos = lax.broadcasted_iota(jnp.int32, (BLOCK, BLOCK), 0)
    col_pos = lax.broadcasted_iota(jnp.int32, (BLOCK, BLOCK), 1)
    return col_pos <= row_pos


def key_ranges(block):
    start = block * BLOCK
    return min(start, PROMPT), start


def attend_kernel(q_ref, k_ref, v_ref, o_ref, lse_ref):
    scale = HD ** (-0.5)
    mask = own_mask()
    for block in range(GROUP // BLOCK):
        far, start = key_ranges(block)
        rows = slice(start, start + BLOCK)
        outs, lses = [], []
        for which in range(2):
            lanes = head_lanes(which)
            q = jnp.where(lanes, q_ref[0, rows, :], 0)
            near = jnp.where(mask, dot(q, k_ref[0, rows, :], 1, 1) * scale, MASKED)
            top = jnp.max(near, axis=-1, keepdims=True)
            if far:
                away = dot(q, k_ref[0, 0:far, :], 1, 1) * scale
                top = jnp.maximum(top, jnp.max(away, axis=-1, keepdims=True))
            near = jnp.exp(near - top)
            total = jnp.sum(near, axis=-1, keepdims=True)
            if far:
                away = jnp.exp(away - top)
                total = total + jnp.sum(away, axis=-1, keepdims=True)
            share = 1.0 / total
            out = dot((near * share).astype(jnp.bfloat16), v_ref[0, rows, :], 1, 0)
            if far:
                out = out + dot((away * share).astype(jnp.bfloat16), v_ref[0, 0:far, :], 1, 0)
            outs.append(out)
            lses.append(top + jnp.log(total))
        first = head_lanes(0)
        o_ref[rows, :] = jnp.where(first, outs[0], outs[1]).astype(jnp.bfloat16)
        lse_ref[rows, :] = jnp.where(first, lses[0], lses[1])


def attend_call(projected):
    _, rows, width = projected.shape
    pairs = width // 128
    spec = [pl.BlockSpec((1, rows, 128), functools.partial(lambda t, i: (t, 0, i), t)) for t in range(3)]
    return pl.pallas_call(
        attend_kernel,
        grid=(pairs,),
        out_shape=(jax.ShapeDtypeStruct((rows, width), jnp.bfloat16),
                   jax.ShapeDtypeStruct((rows, width), jnp.float32)),
        in_specs=spec,
        out_specs=(pl.BlockSpec((rows, 128), lambda i: (0, i)), pl.BlockSpec((rows, 128), lambda i: (0, i))),
        compiler_params=pltpu.CompilerParams(vmem_limit_bytes=48 * 2**20),
        cost_estimate=pl.CostEstimate(flops=4 * 10**9, bytes_accessed=6 * 10**6, transcendentals=4 * 10**6),
        name="attend",
    )(projected, projected, projected)


def attend_back_rows(block, q_ref, k_ref, v_ref, g_ref, lse_ref, dq_ref, dk_ref, dv_ref):
    scale = HD ** (-0.5)
    mask = own_mask()
    low = jnp.bfloat16
    far, start = key_ranges(block)
    rows = slice(start, start + BLOCK)
    dq = None
    for which in range(2):
        lanes = head_lanes(which)
        q = jnp.where(lanes, q_ref[rows, :], 0)
        g = jnp.where(lanes, g_ref[rows, :], 0)
        lse = lse_ref[rows, which * HD : which * HD + 1]
        k_own = jnp.where(lanes, k_ref[rows, :], 0)
        p_own = jnp.where(mask, jnp.exp(dot(q, k_own, 1, 1) * scale - lse), 0.0)
        d_own = dot(g, v_ref[rows, :], 1, 1)
        row_dot = jnp.sum(p_own * d_own, axis=-1, keepdims=True)
        if far:
            k_far = jnp.where(lanes, k_ref[0:far, :], 0)
            p_far = jnp.exp(dot(q, k_far, 1, 1) * scale - lse)
            d_far = dot(g, v_ref[0:far, :], 1, 1)
            row_dot = row_dot + jnp.sum(p_far * d_far, axis=-1, keepdims=True)
        s_own = (p_own * (d_own - row_dot)).astype(low)
        part = dot(s_own, k_own, 1, 0)
        dk_ref[rows, :] += dot(s_own, q, 0, 0)
        dv_ref[rows, :] += dot(p_own.astype(low), g, 0, 0)
        if far:
            s_far = (p_far * (d_far - row_dot)).astype(low)
            part = part + dot(s_far, k_far, 1, 0)
            dk_ref[0:far, :] += dot(s_far, q, 0, 0)
            dv_ref[0:far, :] += dot(p_far.astype(low), g, 0, 0)
        dq = part if dq is None else dq + part
    dq_ref[rows, :] = dq


PAIR_ROWS = 3072


def attend_back_kernel(q_ref, k_ref, v_ref, lse_ref, mixed_ref, cot_ref, ln1_ref, outw_ref, qkvw_ref,
                       part_ref, dn_ref, bias_ref, obias_ref, g_ref, dq_ref, dk_ref, dv_ref, d_ref):
    low, f32 = jnp.bfloat16, jnp.float32
    scale = HD ** (-0.5)
    pair = pl.program_id(0)
    g_ref[...] = dot(cot_ref[...], outw_ref[...], 1, 1).astype(low)
    grad_out = dot(mixed_ref[...], cot_ref[...], 0, 0).astype(low)
    for j in range(6):
        part_ref[j * 128 : (j + 1) * 128, :] = grad_out[:, j * 128 : (j + 1) * 128]
    dk_ref[...] = jnp.zeros_like(dk_ref)
    dv_ref[...] = jnp.zeros_like(dv_ref)
    for block in range(GROUP // BLOCK):
        attend_back_rows(block, q_ref.at[0], k_ref.at[0], v_ref.at[0], g_ref, lse_ref, dq_ref, dk_ref, dv_ref)

    @pl.when(pair == 0)
    def _():
        dn_ref[...] = jnp.zeros_like(dn_ref)
        obias_ref[...] = jnp.sum(cot_ref[...].astype(f32), axis=0, keepdims=True)

    d_ref[0] = (dq_ref[...] * scale).astype(low)
    d_ref[1] = (dk_ref[...] * scale).astype(low)
    d_ref[2] = dv_ref[...].astype(low)
    for t in range(3):
        d = d_ref[t]
        part_ref[(t + 1) * 768 : (t + 2) * 768, :] = dot(ln1_ref[...], d, 0, 0).astype(low)
        dn_ref[...] += dot(d, qkvw_ref[t], 1, 1)
        bias_ref[t : t + 1, :] = jnp.sum(d.astype(f32), axis=0, keepdims=True)


def attend_back_call(projected, lse, mixed, cot, ln1_full, out_weight, qkv_weight):
    _, rows, width = projected.shape
    pairs = width // 128
    depth = cot.shape[1]
    spec = [pl.BlockSpec((1, rows, 128), functools.partial(lambda t, i: (t, 0, i), t)) for t in range(3)]
    column = pl.BlockSpec((rows, 128), lambda i: (0, i))
    whole = pl.BlockSpec((rows, depth), lambda i: (0, 0))
    f32, low = jnp.float32, jnp.bfloat16
    return pl.pallas_call(
        attend_back_kernel,
        grid=(pairs,),
        out_shape=(jax.ShapeDtypeStruct((pairs * PAIR_ROWS, 128), low),
                   jax.ShapeDtypeStruct((rows, depth), f32),
                   jax.ShapeDtypeStruct((3, width), f32),
                   jax.ShapeDtypeStruct((1, depth), f32)),
        in_specs=spec + [column, column, whole, whole,
                         pl.BlockSpec((128, depth), lambda i: (i, 0)),
                         pl.BlockSpec((3, depth, 128), lambda i: (0, 0, i))],
        out_specs=(pl.BlockSpec((PAIR_ROWS, 128), lambda i: (i, 0)), whole,
                   pl.BlockSpec((3, 128), lambda i: (0, i)), pl.BlockSpec((1, depth), lambda i: (0, 0))),
        scratch_shapes=[pltpu.VMEM((rows, 128), low)] + [pltpu.VMEM((rows, 128), f32)] * 3
        + [pltpu.VMEM((3, rows, 128), low)],
        compiler_params=pltpu.CompilerParams(vmem_limit_bytes=56 * 2**20),
        cost_estimate=pl.CostEstimate(flops=12 * 10**9, bytes_accessed=20 * 10**6, transcendentals=4 * 10**6),
        name="attend_back",
    )(projected, projected, projected, lse, mixed, cot, ln1_full, out_weight, qkv_weight)


UNITS = 256


def mlp_kernel(x_ref, g_ref, fcw_ref, fcb_ref, pw_ref, out_ref, dn_ref, pp_ref, fp_ref, fb_ref, pb_ref):
    low, f32 = jnp.bfloat16, jnp.float32
    tile = pl.program_id(0)
    pre = dot(x_ref[...], fcw_ref[...], 1, 0) + fcb_ref[...].astype(f32)
    grad = dot(g_ref[...], pw_ref[...], 1, 1)
    coef = 0.7978845608028654
    square = pre * pre
    curve = jnp.tanh(coef * (pre + 0.044715 * (square * pre)))
    half = 0.5 * (1.0 + curve)
    act = (pre * half).astype(low)
    slope = half + 0.5 * pre * (1.0 - curve * curve) * (coef * (1.0 + 3 * 0.044715 * square))
    d_pre = (grad * slope).astype(low)

    @pl.when(tile == 0)
    def _():
        out_ref[...] = jnp.zeros_like(out_ref)
        dn_ref[...] = jnp.zeros_like(dn_ref)
        pb_ref[...] = jnp.sum(g_ref[...].astype(f32), axis=0, keepdims=True)

    fb_ref[...] = jnp.sum(d_pre.astype(f32), axis=0, keepdims=True)
    grad_proj = dot(act, g_ref[...], 0, 0).astype(low)
    for j in range(6):
        pp_ref[j * UNITS : (j + 1) * UNITS, :] = grad_proj[:, j * 128 : (j + 1) * 128]
    grad_fc = dot(x_ref[...], d_pre, 0, 0).astype(low)
    for j in range(2):
        fp_ref[j * 768 : (j + 1) * 768, :] = grad_fc[:, j * 128 : (j + 1) * 128]
    out_ref[...] += dot(act, pw_ref[...], 1, 0)
    dn_ref[...] += dot(d_pre, fcw_ref[...], 1, 1)


def mlp_call(x, g, fc_weight, fc_bias, proj_weight):
    rows, depth = x.shape
    units = fc_weight.shape[1]
    tiles = units // UNITS
    f32, low = jnp.float32, jnp.bfloat16
    whole = pl.BlockSpec((rows, depth), lambda i: (0, 0))
    item = pl.BlockSpec((ITEM, 128), lambda i: (i, 0))
    return pl.pallas_call(
        mlp_kernel,
        grid=(tiles,),
        out_shape=(jax.ShapeDtypeStruct((rows, depth), f32), jax.ShapeDtypeStruct((rows, depth), f32),
                   jax.ShapeDtypeStruct((tiles * ITEM, 128), low), jax.ShapeDtypeStruct((tiles * ITEM, 128), low),
                   jax.ShapeDtypeStruct((1, units), f32), jax.ShapeDtypeStruct((1, depth), f32)),
        in_specs=[whole, whole, pl.BlockSpec((depth, UNITS), lambda i: (0, i)),
                  pl.BlockSpec((1, UNITS), lambda i: (0, i)), pl.BlockSpec((UNITS, depth), lambda i: (i, 0))],
        out_specs=(whole, whole, item, item, pl.BlockSpec((1, UNITS), lambda i: (0, i)),
                   pl.BlockSpec((1, depth), lambda i: (0, 0))),
        compiler_params=pltpu.CompilerParams(vmem_limit_bytes=60 * 2**20),
        cost_estimate=pl.CostEstimate(flops=17 * 10**9, bytes_accessed=25 * 10**6, transcendentals=2 * 10**6),
        name="mlp",
    )(x, g, fc_weight, fc_bias.reshape(1, units), proj_weight)


def spread_kernel(p_ref, f_ref, proj_ref, fc_ref):
    f32 = jnp.float32
    for j in range(6):
        proj_ref[:, j * 128 : (j + 1) * 128] = p_ref[j * UNITS : (j + 1) * UNITS, :].astype(f32)
    for j in range(2):
        fc_ref[:, j * 128 : (j + 1) * 128] = f_ref[j * 768 : (j + 1) * 768, :].astype(f32)


def spread_call(total, units, depth):
    tiles = units // UNITS
    f32 = jnp.float32
    return pl.pallas_call(
        spread_kernel,
        grid=(tiles,),
        out_shape=(jax.ShapeDtypeStruct((units, depth), f32), jax.ShapeDtypeStruct((depth, units), f32)),
        in_specs=[pl.BlockSpec((ITEM, 128), lambda i: (i, 0)),
                  pl.BlockSpec((ITEM, 128), lambda i: (i + tiles, 0))],
        out_specs=(pl.BlockSpec((UNITS, depth), lambda i: (i, 0)), pl.BlockSpec((depth, UNITS), lambda i: (0, i))),
        compiler_params=pltpu.CompilerParams(vmem_limit_bytes=24 * 2**20),
        name="spread_mlp",
    )(total, total)


def spread_pair_kernel(a_ref, out_ref, qkv_ref):
    f32 = jnp.float32
    for j in range(6):
        out_ref[:, j * 128 : (j + 1) * 128] = a_ref[j * 128 : (j + 1) * 128, :].astype(f32)
    for t in range(3):
        qkv_ref[t] = a_ref[(t + 1) * 768 : (t + 2) * 768, :].astype(f32)


def spread_pair_call(total, first, width, depth):
    pairs = width // 128
    f32 = jnp.float32
    skip = first // PAIR_ROWS
    return pl.pallas_call(
        spread_pair_kernel,
        grid=(pairs,),
        out_shape=(jax.ShapeDtypeStruct((width, depth), f32), jax.ShapeDtypeStruct((3, depth, width), f32)),
        in_specs=[pl.BlockSpec((PAIR_ROWS, 128), lambda i: (i + skip, 0))],
        out_specs=(pl.BlockSpec((128, depth), lambda i: (i, 0)), pl.BlockSpec((3, depth, 128), lambda i: (0, 0, i))),
        compiler_params=pltpu.CompilerParams(vmem_limit_bytes=24 * 2**20),
        name="spread_attend",
    )(total)


def over_slice(values):
    count = lax.axis_size("dp")
    total = values
    for shift in range(16, count, 16):
        total = total + lax.ppermute(values, "dp", [(i, (i + shift) % count) for i in range(count)])
    return total


def on_device(
    tokens,
    ln1_gain,
    ln1_bias,
    qkv_weight,
    qv_bias,
    out_weight,
    out_bias,
    ln2_gain,
    ln2_bias,
    fc_weight,
    fc_bias,
    proj_weight,
    proj_bias,
    cotangent,
):
    own_rows = tokens.shape[0]
    group_rows = own_rows * lax.axis_size("tensor")
    local_width = qkv_weight.shape[2]
    heads_local = local_width // HD
    gain_one = ln1_gain.astype(jnp.float32)
    gain_two = ln2_gain.astype(jnp.float32)
    x_own = tokens.astype(jnp.float32)
    normed1, normal1, inv_std1 = norm_rows(x_own, gain_one, ln1_bias.astype(jnp.float32))
    ln1_full = gather_pair(normed1.astype(jnp.bfloat16))
    projected = jnp.einsum("gd,tdj->tgj", ln1_full, qkv_weight, preferred_element_type=jnp.float32)
    bias_float = qv_bias.astype(jnp.float32)
    bias_rows = jnp.stack([bias_float[0], jnp.zeros_like(bias_float[0]), bias_float[1]])
    projected = (projected + bias_rows[:, None]).astype(jnp.bfloat16)
    mixed_low, lse = attend_call(projected)
    part_rows = mixed_low
    attn_own = scatter_pair(jnp.dot(part_rows, out_weight, preferred_element_type=jnp.float32)) + out_bias.astype(jnp.float32)
    residual = x_own + attn_own
    normed2, normal2, inv_std2 = norm_rows(residual, gain_two, ln2_bias.astype(jnp.float32))
    ln2_full = gather_pair(normed2.astype(jnp.bfloat16))
    cot_full = gather_pair(cotangent)
    mlp_part, norm2_part, part_proj, part_fc, grad_fc_bias, grad_proj_bias = mlp_call(
        ln2_full, cot_full, fc_weight, fc_bias, proj_weight
    )
    block_output = (residual + (scatter_pair(mlp_part) + proj_bias.astype(jnp.float32))).astype(jnp.bfloat16)
    grad_norm2 = scatter_pair(norm2_part)
    grad_resid = cotangent.astype(jnp.float32) + norm_back(grad_norm2, normal2, inv_std2, gain_two)
    part_ln2_gain = jnp.sum(grad_norm2 * normal2, axis=0)
    part_ln2_bias = jnp.sum(grad_norm2, axis=0)
    attn_cot_full = gather_pair(grad_resid.astype(jnp.bfloat16))
    part_attn, norm1_part, grad_bias_rows, grad_out_bias = attend_back_call(
        projected, lse, mixed_low, attn_cot_full, ln1_full, out_weight, qkv_weight
    )
    grad_norm1 = scatter_pair(norm1_part)
    input_grad = (grad_resid + norm_back(grad_norm1, normal1, inv_std1, gain_one)).astype(
        jnp.bfloat16
    )
    part_ln1_gain = jnp.sum(grad_norm1 * normal1, axis=0)
    part_ln1_bias = jnp.sum(grad_norm1, axis=0)
    width = tokens.shape[1]
    units = fc_weight.shape[1]
    small = jnp.concatenate(
        [
            part_ln1_gain,
            part_ln1_bias,
            part_ln2_gain,
            part_ln2_bias,
            grad_bias_rows[0],
            grad_bias_rows[2],
            grad_out_bias[0],
            grad_fc_bias[0],
            grad_proj_bias[0],
            jnp.zeros((SMALL * 128 - 6912,), jnp.float32),
        ]
    ).reshape(SMALL, 128)
    total, small = sum_call((part_proj, part_fc, part_attn), small)
    grad_proj_weight, grad_fc_weight = spread_call(total, units, width)
    grad_out_weight, grad_qkv_weight = spread_pair_call(
        total, 2 * units * width // 128, local_width, width
    )
    small = over_slice(small)
    if lax.axis_size("dp") > 16:
        grad_proj_weight = over_slice(grad_proj_weight)
        grad_fc_weight = over_slice(grad_fc_weight)
        grad_out_weight = over_slice(grad_out_weight)
        grad_qkv_weight = over_slice(grad_qkv_weight)
    flat = small.reshape(-1)
    grad_ln1_gain, grad_ln1_bias = flat[:768], flat[768:1536]
    grad_ln2_gain, grad_ln2_bias = flat[1536:2304], flat[2304:3072]
    grad_qv_bias = flat[3072:3840].reshape(2, local_width)
    grad_out_bias, grad_fc_bias, grad_proj_bias = flat[3840:4608], flat[4608:6144], flat[6144:6912]
    return (
        block_output,
        input_grad,
        grad_ln1_gain,
        grad_ln1_bias,
        grad_qkv_weight,
        grad_qv_bias,
        grad_out_weight,
        grad_out_bias,
        grad_ln2_gain,
        grad_ln2_bias,
        grad_fc_weight,
        grad_fc_bias,
        grad_proj_weight,
        grad_proj_bias,
    )


def solution(mesh):
    return jax.shard_map(
        on_device,
        mesh=mesh,
        in_specs=(
            P(("dp", "tensor"), None),
            P(),
            P(),
            P(None, None, "tensor"),
            P(None, "tensor"),
            P("tensor", None),
            P(),
            P(),
            P(),
            P(None, "tensor"),
            P("tensor"),
            P("tensor", None),
            P(),
            P(("dp", "tensor"), None),
        ),
        out_specs=(
            P(("dp", "tensor"), None),
            P(("dp", "tensor"), None),
            P(),
            P(),
            P(None, None, "tensor"),
            P(None, "tensor"),
            P("tensor", None),
            P(),
            P(),
            P(),
            P(None, "tensor"),
            P("tensor"),
            P("tensor", None),
            P(),
        ),
        check_vma=False,
    )
```

time: 460 us -> 307 us (0.67); the launches traced: 451 us -> 306 us
  matrix products: 116 us -> 3.56 us
  Pallas kernels: 144 us -> 248 us
  local copies, waits for them, and re-layouts: 91.7 us -> 20.7 us
  other arithmetic: 86.9 us -> 16 us
  waiting for transfers between devices: 8.65 us -> 14.5 us
    dot_general x29 -> x1, matrix products: 115 us -> 2.49 us  [on_device(): jnp.einsum('gd,tdj->tgj', ln1_full, qkv_weight, preferred_element_type=jn...]
    pallas_call x0 -> x5, Pallas kernels: none -> 104 us  [the longest x1 45.3 us: attend_back_call(): pl.pallas_call(attend_back_kernel, grid=(pairs,), out_shape=(jax.ShapeDty...]
    concatenate x1 -> x0, other arithmetic: 33.2 us -> none  [on_device(): jnp.concatenate([blocks(grad_proj_weight.astype(low).reshape(units // 256...]
    convert_element_type x4 -> x0, other arithmetic: 19.2 us -> none  [the longest x1 13.5 us: attend_back(): dscore_head = (prob_head * (dprob_head - row_dot)).astype(jnp.bfloat16)]
    unnamed x147 -> x75, local copies, waits for them, and re-layouts: 25.7 us -> 6.55 us
    reduce_sum x6 -> x0, other arithmetic: 13.2 us -> none  [the longest x1 9.03 us: attend_forward(): total_head = jnp.sum(expo_head, axis=-1, keepdims=True)]
    slice x7 -> x1, local copies, waits for them, and re-layouts: 11.1 us -> 0.02 us  [on_device(): grad_bias_rows[2]]
    reshape x7 -> x1, local copies, waits for them, and re-layouts: 10.6 us -> 0.6 us  [mlp_call(): fc_bias.reshape(1, units)]
  transfers between devices with their start and end apart: 8 -> 8, of which waited for: 5 -> 6; matrix products, arithmetic and copies ran while one was open for 13% -> 3% of each run, Pallas kernels for 0% -> 0%
where the time goes in v2:
time: 307 us; the launch traced here: 306 us
  Pallas kernels  248 us (81%)
  local copies, waits for them, and re-layouts  20.7 us (7%)
  other arithmetic  16 us (5%)
  waiting for transfers between devices  14.5 us (5%)
  matrix products  3.56 us (1%)
    pallas_call x1, Pallas kernels, sum_call(): pl.pallas_call(functools.partial(sum_kernel, n), out_shape=(jax.ShapeDtyp...  144 us
    pallas_call x1, Pallas kernels, attend_back_call(): pl.pallas_call(attend_back_kernel, grid=(pairs,), out_shape=(jax.ShapeDty...  45.3 us
    pallas_call x1, Pallas kernels, mlp_call(): pl.pallas_call(mlp_kernel, grid=(tiles,), out_shape=(jax.ShapeDtypeStruct...  28.8 us
    pallas_call x1, Pallas kernels, attend_call(): pl.pallas_call(attend_kernel, grid=(pairs,), out_shape=(jax.ShapeDtypeStr...  23.5 us
    ppermute x8, waiting for transfers between devices, swap(): return lax.ppermute(values, 'tensor', [(0, 1), (1, 0)])  14.5 us
    unnamed x75, local copies, waits for them, and re-layouts  6.55 us
  transfers between devices with their start and end apart: 8, of which 6 were waited for; matrix products, arithmetic and copies ran while one was open for 3% of the time, Pallas kernels for 0%

profile of v2, /device:TPU:0, one launch (start us, length us, event | category | flops | bytes accessed | tf_op | source)
XLA Modules:
  0.0 306.4 jit_solution(14927943945029960231)
XLA Ops:
  0.7 1.4 convert_reduce_fusion
  2.2 1.6 fusion.15
  3.9 0.4 constant_dynamic-update-slice_fusion.17
  4.4 0.6 collective-permute-start
  5.0 0.8 fusion.19
  5.9 1.1 collective-permute-done
  7.1 2.5 fusion.q_ref.k_ref.v_ref
  9.6 23.5 %attend.1 = (bf16[1152,384]{1,0:T(8,128)(2,1)S(1)}, f32[1152,384]{1,0:T(8,128)S(1)}) custom-call(bf16[3,1152,384]{2,1,0:T(8,128)(2,1)S(1)} %fusion.q_ref.k_ref.v_ref, bf16[3,1152,384]{2,1,0:T(8,128)(2,1)S(1)} %fusion.q_ref.k_ref.v_ref, bf16[3,1152,384]{2,1,0:T(8,128)(2,1)S(1)} %fusion.q_ref.k_ref.v_ref), custom_call_target="tpu_custom_call" | custom-call | flops 4000000000 | bytes 6000000 | tf_op jit(solution)/shard_map/attend/pallas_call | solution.py:323
  33.1 1.1 fusion.20
  34.2 0.4 copy-done.3
  34.8 0.4 collective-permute-start.1
  35.2 0.6 copy-done.7
  35.8 0.4 collective-permute-start.3
  36.2 2.3 collective-permute-done.1
  38.5 0.4 fusion.17
  39.0 0.3 multiply_reduce_fusion.2
  39.3 1.3 broadcast.75.clone.1
  40.7 1.3 constant_dynamic-update-slice_fusion.15
  41.9 0.4 collective-permute-start.2
  42.3 0.6 reshape.94.fcb_ref
  42.9 1.4 broadcast.75.clone.2
  44.3 1.0 constant_dynamic-update-slice_fusion.13
  45.3 1.0 constant_dynamic-update-slice_fusion.12.g_ref
  46.3 1.0 constant_dynamic-update-slice_fusion.14.x_ref
  47.2 28.8 %mlp.1 = (f32[1152,768]{1,0:T(8,128)}, f32[1152,768]{1,0:T(8,128)}, bf16[9216,128]{1,0:T(8,128)(2,1)}, bf16[9216,128]{1,0:T(8,128)(2,1)}, f32[1,1536]{1,0:T(1,128)}, /*index=5*/f32[1,768]{1,0:T(1,128)}) custom-call(bf16[1152,768]{1,0:T(8,128)(2,1)} %constant_dynamic-update-slice_fusion.14.x_ref, ...), custom_call_target="tpu_custom_call" | custom-call | flops 16999999488 | bytes 25000000 | tf_op jit(solution)/shard_map/mlp/pallas_call | solution.py:470
  76.1 1.7 constant_dynamic-slice_fusion.2
  77.8 0.2 collective-permute-start.4
  78.0 0.5 copy-done.9
  78.7 0.2 collective-permute-start.5
  78.9 2.7 collective-permute-done.4
  81.6 2.5 collective-permute-done.5
  84.1 2.0 multiply_reduce_fusion
  86.2 2.0 constant_dynamic-update-slice_fusion.11
  88.4 2.3 collective-permute-done.6
  90.7 1.2 copy-done.10
  91.9 45.3 %attend_back.1 = (bf16[9216,128]{1,0:T(8,128)(2,1)}, f32[1152,768]{1,0:T(8,128)}, f32[3,384]{1,0:T(4,128)}, f32[1,768]{1,0:T(1,128)}) custom-call(bf16[3,1152,384]{2,1,0:T(8,128)(2,1)} %copy-done.2, bf16[3,1152,384]{2,1,0:T(8,128)(2,1)} %copy-done.2, bf16[3,1152,384]{2,1,0:T(8,128)(2,1)} %copy-done.2, f32[1152,384]{1,0:T(8,128)} %copy-done.3, ...), custom_call_target="tpu_custom_call" | custom-call | flops 12000000000 | bytes 20000000 | tf_op jit(solution)/shard_map/attend_back/pallas_call | solution.py:410
  137.3 2.8 constant_dynamic-slice_fusion
  140.4 3.6 %collective-permute-done.7 = f32[576,768]{1,0:T(8,128)S(1)} collective-permute-done((f32[576,768]{1,0:T(8,128)}, f32[576,768]{1,0:T(8,128)S(1)}, u32[]{:S(2)}, u32[]{:S(2)}) %collective-permute-start.7) | collective-permute-done | bytes 1769504 | tf_op jit(solution)/shard_map/ppermute | solution.py:244
  144.0 3.4 %fusion.14 = (f32[768]{0:T(1024)S(1)}, f32[576]{0:T(1024)S(1)}, f32[576]{0:T(1024)S(1)}, f32[768]{0:T(1024)S(1)}, f32[576,768]{1,0:T(8,128)}) fusion(bf16[576,768]{1,0:T(8,128)(2,1)S(1)} %copy-done.5, f32[576]{0:T(1024)S(1)} %copy-done.16, f32[576]{0:T(1024)S(1)} %copy-done.14, f32[768]{0:T(1024)S(1)} %copy-done.18, ...), kind=kLoop, calls=%fused_computation.18 | loop fusion | flops 4863360 | bytes 6211588 | tf_op jit(solution)/shard_map/reduce_sum | solution.py:592
  147.5 0.6 copy-done.20
  148.1 143.9 %grad_sum.1 = (bf16[27648,128]{1,0:T(8,128)(2,1)}, f32[56,128]{1,0:T(8,128)}) custom-call(bf16[9216,128]{1,0:T(8,128)(2,1)} %get-tuple-element.37.refs_0_, bf16[9216,128]{1,0:T(8,128)(2,1)} %get-tuple-element.38.refs_1_, bf16[9216,128]{1,0:T(8,128)(2,1)} %get-tuple-element.39.refs_2_, f32[56,128]{1,0:T(8,128)} %bitcast.24), custom_call_target="tpu_custom_call" | custom-call | tf_op jit(solution)/shard_map/grad_sum/pallas_call | solution.py:216
  292.0 3.0 copy-done
  295.0 4.1 %spread_mlp.1 = (f32[1536,768]{1,0:T(8,128)}, f32[768,1536]{1,0:T(8,128)}) custom-call(bf16[27648,128]{1,0:T(8,128)(2,1)S(1)} %copy-done, bf16[27648,128]{1,0:T(8,128)(2,1)S(1)} %copy-done), custom_call_target="tpu_custom_call" | custom-call | tf_op jit(solution)/shard_map/spread_mlp/pallas_call | solution.py:497
  299.1 2.4 spread_attend.1
  301.5 0.6 slice_bitcast_fusion.1
  302.2 0.6 slice_bitcast_fusion
  302.8 0.6 reshape.96
  303.4 3.0 fusion.13
  (100 shorter events, 1.4 us)
Async XLA Ops:
  0.6 3.1 %copy-start.25 = (bf16[768]{0:T(1024)(128)(2,1)S(1)}, bf16[768]{0:T(1024)(128)(2,1)}, u32[]{:S(2)}) copy-start(bf16[768]{0:T(1024)(128)(2,1)} %param.15) | copy-start | bytes 4612
  0.7 3.1 %copy-start.26 = (bf16[768]{0:T(1024)(128)(2,1)S(1)}, bf16[768]{0:T(1024)(128)(2,1)}, u32[]{:S(2)}) copy-start(bf16[768]{0:T(1024)(128)(2,1)} %param.16) | copy-start | bytes 4612
  0.7 3.3 %copy-start.4 = (bf16[576,768]{1,0:T(8,128)(2,1)S(1)}, bf16[576,768]{1,0:T(8,128)(2,1)}, u32[]{:S(2)}) copy-start(bf16[576,768]{1,0:T(8,128)(2,1)} %param.14) | copy-start | bytes 2654212
  2.1 2.2 copy-start.13
  3.7 0.6 copy-start.15
  3.8 0.6 copy-start.17
  4.4 2.6 collective-permute-start
  4.9 2.1 copy-start.32
  7.1 2.5 copy-start.11
  9.6 23.5 %copy-start.2 = (bf16[3,1152,384]{2,1,0:T(8,128)(2,1)}, bf16[3,1152,384]{2,1,0:T(8,128)(2,1)S(1)}, u32[]{:S(2)}) copy-start(bf16[3,1152,384]{2,1,0:T(8,128)(2,1)S(1)} %fusion.q_ref.k_ref.v_ref) | copy-start | bytes 7962628
  9.6 23.5 %copy-start.12 = (bf16[384,768]{1,0:T(8,128)(2,1)S(1)}, bf16[384,768]{1,0:T(8,128)(2,1)}, u32[]{:S(2)}) copy-start(bf16[384,768]{1,0:T(8,128)(2,1)} %outw_ref.1) | copy-start | bytes 1769476
  33.1 1.1 copy-start.1
  33.1 1.5 copy-start.3
  34.6 1.2 copy-start.7
  34.6 1.5 copy-start.27
  34.6 1.5 copy-start.28
  34.6 1.6 copy-start.29
  34.6 3.9 %copy-start.5 = (bf16[576,768]{1,0:T(8,128)(2,1)S(1)}, bf16[576,768]{1,0:T(8,128)(2,1)}, u32[]{:S(2)}) copy-start(bf16[576,768]{1,0:T(8,128)(2,1)} %param.14) | copy-start | bytes 2654212
  34.8 3.8 %collective-permute-start.1 = (f32[576,768]{1,0:T(8,128)S(1)}, f32[576,768]{1,0:T(8,128)S(1)}, u32[]{:S(2)}, u32[]{:S(2)}) collective-permute-start(f32[576,768]{1,0:T(8,128)S(1)} %constant_dynamic-slice_fusion.3), channel_id=1, source_target_pairs={{0,1},{1,0},{2,3},{3,2},{4,5},{5,4},{6,7},{7,6},{8,9},{9,8},{10,11... | collective-permute-start | bytes 5308424 | tf_op jit(solution)/shard_map/ppermute | solution.py:244
  35.8 9.5 %collective-permute-start.3 = (bf16[576,768]{1,0:T(8,128)(2,1)S(1)}, bf16[576,768]{1,0:T(8,128)(2,1)S(1)}, u32[]{:S(2)}, u32[]{:S(2)}) collective-permute-start(bf16[576,768]{1,0:T(8,128)(2,1)S(1)} %copy-done.7), channel_id=1, source_target_pairs={{0,1},{1,0},{2,3},{3,2},{4,5},{5,4},{6,7},{7,6},{8,9},{9,8},{10,11... | collective-permute-start | bytes 2654216 | tf_op jit(solution)/shard_map/ppermute | solution.py:244
  40.7 1.6 copy-start.22
  41.9 4.3 %collective-permute-start.2 = (bf16[576,768]{1,0:T(8,128)(2,1)S(1)}, bf16[576,768]{1,0:T(8,128)(2,1)S(1)}, u32[]{:S(2)}, u32[]{:S(2)}) collective-permute-start(bf16[576,768]{1,0:T(8,128)(2,1)S(1)} %get-tuple-element.66), channel_id=1, source_target_pairs={{0,1},{1,0},{2,3},{3,2},{4,5},{5,4},{6,7},{7,6},{8,9},{9,8},{10,11... | collective-permute-start | bytes 2654216 | tf_op jit(solution)/shard_map/ppermute | solution.py:244
  76.1 2.5 copy-start.9
  76.1 2.9 copy-start.30
  77.8 3.8 %collective-permute-start.4 = (f32[576,768]{1,0:T(8,128)S(1)}, f32[576,768]{1,0:T(8,128)S(1)}, u32[]{:S(2)}, u32[]{:S(2)}) collective-permute-start(f32[576,768]{1,0:T(8,128)S(1)} %constant_dynamic-slice_fusion.2), channel_id=1, source_target_pairs={{0,1},{1,0},{2,3},{3,2},{4,5},{5,4},{6,7},{7,6},{8,9},{9,8},{10,11... | collective-permute-start | bytes 5308424 | tf_op jit(solution)/shard_map/ppermute | solution.py:244
  78.6 5.5 %copy-start.8 = (f32[1152,768]{1,0:T(8,128)S(1)}, f32[1152,768]{1,0:T(8,128)}, u32[]{:S(2)}) copy-start(f32[1152,768]{1,0:T(8,128)} %get-tuple-element.33) | copy-start | bytes 10616836
  78.7 5.4 %collective-permute-start.5 = (f32[576,768]{1,0:T(8,128)S(1)}, f32[576,768]{1,0:T(8,128)S(1)}, u32[]{:S(2)}, u32[]{:S(2)}) collective-permute-start(f32[576,768]{1,0:T(8,128)S(1)} %constant_dynamic-slice_fusion.1), channel_id=1, source_target_pairs={{0,1},{1,0},{2,3},{3,2},{4,5},{5,4},{6,7},{7,6},{8,9},{9,8},{10,11... | collective-permute-start | bytes 5308424 | tf_op jit(solution)/shard_map/ppermute | solution.py:244
  88.2 2.4 collective-permute-start.6
  90.7 1.2 copy-start.10
  137.2 3.1 copy-start.21
  137.2 3.1 %copy-start.23 = (f32[1,768]{1,0:T(1,128)S(1)}, f32[1,768]{1,0:T(1,128)}, u32[]{:S(2)}) copy-start(f32[1,768]{1,0:T(1,128)} %get-tuple-element.43) | copy-start | bytes 9220
  137.2 3.1 %copy-start.24 = (f32[1,768]{1,0:T(1,128)S(1)}, f32[1,768]{1,0:T(1,128)}, u32[]{:S(2)}) copy-start(f32[1,768]{1,0:T(1,128)} %get-tuple-element.41) | copy-start | bytes 9220
  137.2 3.1 %copy-start.31 = (f32[3,384]{1,0:T(4,128)S(1)}, f32[3,384]{1,0:T(4,128)}, u32[]{:S(2)}) copy-start(f32[3,384]{1,0:T(4,128)} %get-tuple-element.40) | copy-start | bytes 13828
  137.3 6.8 %copy-start.14 = (f32[576]{0:T(1024)S(1)}, f32[576]{0:T(1024)}, u32[]{:S(2)}) copy-start(f32[576]{0:T(1024)} %copy-done.13) | copy-start | bytes 6916
  137.3 6.8 %copy-start.16 = (f32[576]{0:T(1024)S(1)}, f32[576]{0:T(1024)}, u32[]{:S(2)}) copy-start(f32[576]{0:T(1024)} %copy-done.15) | copy-start | bytes 6916
  137.3 6.7 %copy-start.18 = (f32[768]{0:T(1024)S(1)}, f32[768]{0:T(1024)}, u32[]{:S(2)}) copy-start(f32[768]{0:T(1024)} %copy-done.17) | copy-start | bytes 9220
  140.1 3.9 %collective-permute-start.7 = (f32[576,768]{1,0:T(8,128)}, f32[576,768]{1,0:T(8,128)S(1)}, u32[]{:S(2)}, u32[]{:S(2)}) collective-permute-start(f32[576,768]{1,0:T(8,128)} %constant_dynamic-slice_fusion), channel_id=1, source_target_pairs={{0,1},{1,0},{2,3},{3,2},{4,5},{5,4},{6,7},{7,6},{8,9},{9,8},{10,11... | collective-permute-start | bytes 5308424 | tf_op jit(solution)/shard_map/ppermute | solution.py:244
  147.5 0.6 copy-start.20
  292.0 3.0 copy-start
  299.1 2.5 copy-start.19
  299.1 4.3 %copy-start.6 = (f32[576,768]{1,0:T(8,128)S(1)}, f32[576,768]{1,0:T(8,128)}, u32[]{:S(2)}) copy-start(f32[576,768]{1,0:T(8,128)} %get-tuple-element.63) | copy-start | bytes 5308420

commit v3 on v2

--- a/solution.py
+++ b/solution.py
@@ -42,9 +42,9 @@
 
 
 class Sum:
-    def __init__(self, part, res, rx1, rx2, rx3, ssem, rsem):
+    def __init__(self, part, res, rx1, rx2, rx3, ssem, rsem, loc):
         self.part, self.res, self.rx1, self.rx2, self.rx3 = part, res, rx1, rx2, rx3
-        self.ssem, self.rsem = ssem, rsem
+        self.ssem, self.rsem, self.loc = ssem, rsem, loc
         dp, t = lax.axis_index("dp"), lax.axis_index("tensor")
         x, y, z = lax.rem(dp, 2), lax.rem(lax.div(dp, 2), 2), lax.rem(lax.div(dp, 4), 4)
         self.t, self.z = t, z
@@ -96,13 +96,18 @@
                 out.append(self.copy(src, dst, 2 + d, i, self.to_z[d]))
             return out
         if stage == 4:
-            ref = self.res.at[self.rows(block, ITEM // 16)]
-            return [self.copy(ref, ref, 5 + d, i, self.to_z[d]) for d in range(3)]
+            own = self.rows(block, ITEM // 16)
+            return [self.copy(self.part.at[own], self.res.at[own], 5 + d, i, self.to_z[d]) for d in range(3)]
         if stage == 5:
             ref = self.res.at[self.rows(quarter, ITEM // 4)]
             return [self.copy(ref, ref, 8, i, self.to_b)]
         ref = self.res.at[self.rows(half, ITEM // 2)]
         return [self.copy(ref, ref, 9, i, self.to_a)]
+
+    def keep(self, i):
+        own = self.rows(
+            i * ITEM + self.a * (ITEM // 2) + self.b * (ITEM // 4) + self.z * (ITEM // 16), ITEM // 16)
+        return pltpu.make_async_copy(self.part.at[own], self.res.at[own], self.loc.at[i])
 
     def start(self, stage, i):
         for c in self.copies(stage, i):
@@ -128,7 +133,10 @@
             total = self.part[own, :].astype(f32)
             for d in range(3):
                 total = total + self.rx3[self.rows((i * 3 + d) * (ITEM // 16), ITEM // 16), :].astype(f32)
-            self.res[own, :] = total.astype(jnp.bfloat16)
+            self.part[own, :] = total.astype(jnp.bfloat16)
+            self.keep(i).start()
+        elif stage == 4:
+            self.keep(i).wait()
         if stage < 6:
             self.start(stage + 1, i)
 
@@ -172,72 +180,6 @@
     for s in [c, cx, cy] + cz:
         s.wait_send()
     yield
-
-
-def sum_kernel(n, *refs):
-    (part_p, part_f, part_a, small, res, small_out, part, rx1, rx2, rx3, ssem, rsem,
-     land_c, land_x, land_y, land_z, acc, ss, sr, lsem) = refs
-    comm = Sum(part, res, rx1, rx2, rx3, ssem, rsem)
-    third = n // 3 * ITEM
-    loads = [
-        pltpu.make_async_copy(ref, part.at[pl.ds(k * third, third)], lsem.at[k])
-        for k, ref in enumerate((part_p, part_f, part_a))
-    ]
-    for load in loads:
-        load.start()
-    comm.barrier()
-    for load in loads:
-        load.wait()
-    sm = small_sum(comm, small, small_out, land_c, land_x, land_y, land_z, acc, ss, sr)
-    next(sm)
-    lax.fori_loop(0, n, lambda i, c: (comm.start(1, i), c)[1], 0)
-    next(sm)
-
-    def step(s, c):
-        for stage in range(1, 7):
-            i = s - (stage - 1)
-
-            @pl.when((i >= 0) & (i < n))
-            def _():
-                comm.arrive(stage, i)
-        return c
-
-    lax.fori_loop(0, n + 5, step, 0)
-    next(sm)
-    next(sm)
-    next(sm)
-    lax.fori_loop(0, n, lambda i, c: (comm.sent(i), c)[1], 0)
-
-
-def sum_call(parts, small):
-    shape = (sum(part.shape[0] for part in parts), 128)
-    n = shape[0] // ITEM
-    f32, bf = jnp.float32, jnp.bfloat16
-    return pl.pallas_call(
-        functools.partial(sum_kernel, n),
-        out_shape=(jax.ShapeDtypeStruct(shape, bf), jax.ShapeDtypeStruct(small.shape, f32)),
-        in_specs=[pl.BlockSpec(memory_space=pl.ANY)] * 3 + [pl.BlockSpec(memory_space=pltpu.VMEM)],
-        out_specs=(pl.BlockSpec(memory_space=pltpu.VMEM), pl.BlockSpec(memory_space=pltpu.VMEM)),
-        scratch_shapes=[
-            pltpu.VMEM(shape, bf),
-            pltpu.VMEM((n * ITEM // 2, 128), bf),
-            pltpu.VMEM((n * ITEM // 4, 128), bf),
-            pltpu.VMEM((n * 3 * ITEM // 16, 128), bf),
-            pltpu.SemaphoreType.DMA((10, n)),
-            pltpu.SemaphoreType.DMA((10, n)),
-            pltpu.VMEM((LN_ROWS, 128), f32),
-            pltpu.VMEM((SMALL, 128), f32),
-            pltpu.VMEM((SMALL, 128), f32),
-            pltpu.VMEM((4, SMALL, 128), f32),
-            pltpu.VMEM((3, SMALL, 128), f32),
-            pltpu.SemaphoreType.DMA((6,)),
-            pltpu.SemaphoreType.DMA((6,)),
-            pltpu.SemaphoreType.DMA((3,)),
-        ],
-        compiler_params=pltpu.CompilerParams(
-            collective_id=0, has_side_effects=True, vmem_limit_bytes=56 * 2**20),
-        name="grad_sum",
-    )(*parts, small)
 
 
 def swap(values):
@@ -370,117 +312,232 @@
 PAIR_ROWS = 3072
 
 
-def attend_back_kernel(q_ref, k_ref, v_ref, lse_ref, mixed_ref, cot_ref, ln1_ref, outw_ref, qkvw_ref,
-                       part_ref, dn_ref, bias_ref, obias_ref, g_ref, dq_ref, dk_ref, dv_ref, d_ref):
-    low, f32 = jnp.bfloat16, jnp.float32
-    scale = HD ** (-0.5)
-    pair = pl.program_id(0)
-    g_ref[...] = dot(cot_ref[...], outw_ref[...], 1, 1).astype(low)
-    grad_out = dot(mixed_ref[...], cot_ref[...], 0, 0).astype(low)
-    for j in range(6):
-        part_ref[j * 128 : (j + 1) * 128, :] = grad_out[:, j * 128 : (j + 1) * 128]
-    dk_ref[...] = jnp.zeros_like(dk_ref)
-    dv_ref[...] = jnp.zeros_like(dv_ref)
-    for block in range(GROUP // BLOCK):
-        attend_back_rows(block, q_ref.at[0], k_ref.at[0], v_ref.at[0], g_ref, lse_ref, dq_ref, dk_ref, dv_ref)
-
-    @pl.when(pair == 0)
-    def _():
-        dn_ref[...] = jnp.zeros_like(dn_ref)
-        obias_ref[...] = jnp.sum(cot_ref[...].astype(f32), axis=0, keepdims=True)
-
-    d_ref[0] = (dq_ref[...] * scale).astype(low)
-    d_ref[1] = (dk_ref[...] * scale).astype(low)
-    d_ref[2] = dv_ref[...].astype(low)
-    for t in range(3):
-        d = d_ref[t]
-        part_ref[(t + 1) * 768 : (t + 2) * 768, :] = dot(ln1_ref[...], d, 0, 0).astype(low)
-        dn_ref[...] += dot(d, qkvw_ref[t], 1, 1)
-        bias_ref[t : t + 1, :] = jnp.sum(d.astype(f32), axis=0, keepdims=True)
-
-
-def attend_back_call(projected, lse, mixed, cot, ln1_full, out_weight, qkv_weight):
-    _, rows, width = projected.shape
-    pairs = width // 128
-    depth = cot.shape[1]
-    spec = [pl.BlockSpec((1, rows, 128), functools.partial(lambda t, i: (t, 0, i), t)) for t in range(3)]
-    column = pl.BlockSpec((rows, 128), lambda i: (0, i))
-    whole = pl.BlockSpec((rows, depth), lambda i: (0, 0))
-    f32, low = jnp.float32, jnp.bfloat16
-    return pl.pallas_call(
-        attend_back_kernel,
-        grid=(pairs,),
-        out_shape=(jax.ShapeDtypeStruct((pairs * PAIR_ROWS, 128), low),
-                   jax.ShapeDtypeStruct((rows, depth), f32),
-                   jax.ShapeDtypeStruct((3, width), f32),
-                   jax.ShapeDtypeStruct((1, depth), f32)),
-        in_specs=spec + [column, column, whole, whole,
-                         pl.BlockSpec((128, depth), lambda i: (i, 0)),
-                         pl.BlockSpec((3, depth, 128), lambda i: (0, 0, i))],
-        out_specs=(pl.BlockSpec((PAIR_ROWS, 128), lambda i: (i, 0)), whole,
-                   pl.BlockSpec((3, 128), lambda i: (0, i)), pl.BlockSpec((1, depth), lambda i: (0, 0))),
-        scratch_shapes=[pltpu.VMEM((rows, 128), low)] + [pltpu.VMEM((rows, 128), f32)] * 3
-        + [pltpu.VMEM((3, rows, 128), low)],
-        compiler_params=pltpu.CompilerParams(vmem_limit_bytes=56 * 2**20),
-        cost_estimate=pl.CostEstimate(flops=12 * 10**9, bytes_accessed=20 * 10**6, transcendentals=4 * 10**6),
-        name="attend_back",
-    )(projected, projected, projected, lse, mixed, cot, ln1_full, out_weight, qkv_weight)
-
-
 UNITS = 256
 
 
-def mlp_kernel(x_ref, g_ref, fcw_ref, fcb_ref, pw_ref, out_ref, dn_ref, pp_ref, fp_ref, fb_ref, pb_ref):
-    low, f32 = jnp.bfloat16, jnp.float32
-    tile = pl.program_id(0)
-    pre = dot(x_ref[...], fcw_ref[...], 1, 0) + fcb_ref[...].astype(f32)
-    grad = dot(g_ref[...], pw_ref[...], 1, 1)
+LAG = 3
+
+
+def column_sum(values):
+    return jnp.sum(values, axis=0, keepdims=True)
+
+
+def put_vector(small, row, vector):
+    for j in range(vector.shape[1] // 128):
+        small[row + j : row + j + 1, :] = vector[:, j * 128 : (j + 1) * 128]
+
+
+def slope_and_act(pre):
     coef = 0.7978845608028654
     square = pre * pre
     curve = jnp.tanh(coef * (pre + 0.044715 * (square * pre)))
     half = 0.5 * (1.0 + curve)
-    act = (pre * half).astype(low)
     slope = half + 0.5 * pre * (1.0 - curve * curve) * (coef * (1.0 + 3 * 0.044715 * square))
-    d_pre = (grad * slope).astype(low)
-
-    @pl.when(tile == 0)
-    def _():
-        out_ref[...] = jnp.zeros_like(out_ref)
-        dn_ref[...] = jnp.zeros_like(dn_ref)
-        pb_ref[...] = jnp.sum(g_ref[...].astype(f32), axis=0, keepdims=True)
-
-    fb_ref[...] = jnp.sum(d_pre.astype(f32), axis=0, keepdims=True)
-    grad_proj = dot(act, g_ref[...], 0, 0).astype(low)
-    for j in range(6):
-        pp_ref[j * UNITS : (j + 1) * UNITS, :] = grad_proj[:, j * 128 : (j + 1) * 128]
-    grad_fc = dot(x_ref[...], d_pre, 0, 0).astype(low)
-    for j in range(2):
-        fp_ref[j * 768 : (j + 1) * 768, :] = grad_fc[:, j * 128 : (j + 1) * 128]
-    out_ref[...] += dot(act, pw_ref[...], 1, 0)
-    dn_ref[...] += dot(d_pre, fcw_ref[...], 1, 1)
-
-
-def mlp_call(x, g, fc_weight, fc_bias, proj_weight):
+    return slope, pre * half
+
+
+def back_kernel(n, tiles, pairs, *refs):
+    (x_ref, g_ref, fcw_in, fcb_ref, pw_in, pb_ref, gain1, gain2, outw_in, qkvw_in, qkv_in, lse_in, mixed_in, ln1_in,
+     resid_in, tok_in,
+     res, small_out, block_out, input_out,
+     fcw_ref, pw_ref, outw_ref, qkvw_ref, qkv_ref, lse_ref, mixed_ref, ln1_ref, resid_ref, tok_ref, lsem,
+     act_ref, dpre_ref, acc0, acc1, land0, land1, dattn, gresid, dm_ref, dq_ref, dk_ref, dv_ref, d_ref,
+     part, rx1, rx2, rx3, ssem, rsem, loc, psem_s, psem_r,
+     small, land_c, land_x, land_y, land_z, sacc, ss, sr) = refs
+    low, f32 = jnp.bfloat16, jnp.float32
+    scale = HD ** (-0.5)
+    comm = Sum(part, res, rx1, rx2, rx3, ssem, rsem, loc)
+    loads = [
+        pltpu.make_async_copy(src, dst, lsem.at[k])
+        for k, (src, dst) in enumerate((
+            (fcw_in, fcw_ref), (pw_in, pw_ref), (resid_in, resid_ref), (outw_in, outw_ref), (mixed_in, mixed_ref),
+            (qkv_in, qkv_ref), (lse_in, lse_ref), (ln1_in, ln1_ref), (qkvw_in, qkvw_ref), (tok_in, tok_ref)))
+    ]
+    for load in loads:
+        load.start()
+    comm.barrier()
+    rows, depth = x_ref.shape
+    own_rows = rows // 2
+    own = pl.ds(pl.multiple_of(comm.t * own_rows, 64), own_rows)
+    away = pl.ds(pl.multiple_of((1 - comm.t) * own_rows, 64), own_rows)
+
+    def pair_copy(src, dst, k):
+        return pltpu.make_async_remote_copy(
+            src_ref=src, dst_ref=dst, send_sem=psem_s.at[k], recv_sem=psem_r.at[k],
+            device_id=comm.to_c, device_id_type=MESH)
+
+    def wave(w):
+        for stage in range(1, 7):
+            i = w - (stage - 1)
+
+            @pl.when((i >= 0) & (i < n))
+            def _():
+                comm.arrive(stage, i)
+
+    small[...] = jnp.zeros_like(small)
+    put_vector(small, 48, column_sum(g_ref[...].astype(f32)))
+    acc0[...] = jnp.zeros_like(acc0)
+    acc1[...] = jnp.zeros_like(acc1)
+    loads[0].wait()
+    loads[1].wait()
+
+    def tile_step(k, carry):
+        units = pl.ds(pl.multiple_of(k * UNITS, UNITS), UNITS)
+        bias = fcb_ref[0:1, units].astype(f32)
+        for part_rows in range(2):
+            chunk = slice(part_rows * own_rows, (part_rows + 1) * own_rows)
+            pre = dot(x_ref[chunk, :], fcw_ref[:, units], 1, 0) + bias
+            slope, act = slope_and_act(pre)
+            act_ref[chunk, :] = act.astype(low)
+            dpre_ref[chunk, :] = (dot(g_ref[chunk, :], pw_ref[units, :], 1, 1) * slope).astype(low)
+        base = pl.multiple_of(k * 2 * ITEM, ITEM)
+        grad_proj = dot(act_ref[...], g_ref[...], 0, 0).astype(low)
+        for j in range(6):
+            part[pl.ds(base + j * UNITS, UNITS), :] = grad_proj[:, j * 128 : (j + 1) * 128]
+        grad_fc = dot(x_ref[...], dpre_ref[...], 0, 0).astype(low)
+        for j in range(2):
+            part[pl.ds(base + ITEM + j * 768, 768), :] = grad_fc[:, j * 128 : (j + 1) * 128]
+        comm.start(1, 2 * k)
+        comm.start(1, 2 * k + 1)
+        sums = column_sum(dpre_ref[...].astype(f32))
+        for j in range(2):
+            small[pl.ds(36 + 2 * k + j, 1), :] = sums[:, j * 128 : (j + 1) * 128]
+        for part_rows in range(2):
+            chunk = slice(part_rows * own_rows, (part_rows + 1) * own_rows)
+            acc1[chunk, :] += dot(dpre_ref[chunk, :], fcw_ref[:, units], 1, 1)
+            acc0[chunk, :] += dot(act_ref[chunk, :], pw_ref[units, :], 1, 0)
+        wave(k - LAG)
+        return carry
+
+    lax.fori_loop(0, tiles, tile_step, 0)
+    send_dn = pair_copy(acc1.at[away], land1, 0)
+    send_dn.start()
+    send_out = pair_copy(acc0.at[away], land0, 1)
+    send_out.start()
+    loads[2].wait()
+    gain = gain2[0:1, :].astype(f32)
+    cot = g_ref[own, :].astype(f32)
+    send_dn.wait_recv()
+    resid = resid_ref[...]
+    centred = resid - jnp.mean(resid, axis=-1, keepdims=True)
+    inv_std = lax.rsqrt(jnp.mean(centred * centred, axis=-1, keepdims=True) + EPSILON)
+    normal = centred * inv_std
+    grad_norm = acc1[own, :] + land1[...]
+    put_vector(small, 12, column_sum(grad_norm * normal))
+    put_vector(small, 18, column_sum(grad_norm))
+    gresid[...] = cot + norm_back(grad_norm, normal, inv_std, gain)
+    dattn[own, :] = gresid[...].astype(low)
+    send_cot = pair_copy(dattn.at[own], dattn.at[own], 2)
+    send_cot.start()
+    send_out.wait_recv()
+    block_out[...] = (resid_ref[...] + (acc0[own, :] + land0[...] + pb_ref[0:1, :].astype(f32))).astype(low)
+    send_out.wait_send()
+    send_dn.wait_send()
+    for load in loads[3:]:
+        load.wait()
+    acc0[...] = jnp.zeros_like(acc0)
+    pair_copy(dattn.at[away], dattn.at[away], 2).wait_recv()
+    put_vector(small, 30, column_sum(dattn[...].astype(f32)))
+
+    def pair_step(p, carry):
+        lanes = pl.ds(pl.multiple_of(p * 128, 128), 128)
+        dm_ref[...] = dot(dattn[...], outw_ref[pl.ds(pl.multiple_of(p * 128, 128), 128), :], 1, 1).astype(low)
+        base = pl.multiple_of(2 * tiles * ITEM + p * PAIR_ROWS, ITEM)
+        grad_out = dot(mixed_ref[:, lanes], dattn[...], 0, 0).astype(low)
+        for j in range(6):
+            part[pl.ds(base + j * 128, 128), :] = grad_out[:, j * 128 : (j + 1) * 128]
+        dk_ref[...] = jnp.zeros_like(dk_ref)
+        dv_ref[...] = jnp.zeros_like(dv_ref)
+        views = [qkv_ref.at[t, :, lanes] for t in range(3)] + [dm_ref, lse_ref.at[:, lanes]]
+        for block in range(GROUP // BLOCK):
+            attend_back_rows(block, *views, dq_ref, dk_ref, dv_ref)
+            if block % 3 == 2:
+                wave(tiles - LAG + 3 * p + block // 3)
+        d_ref[0] = (dq_ref[...] * scale).astype(low)
+        d_ref[1] = (dk_ref[...] * scale).astype(low)
+        d_ref[2] = dv_ref[...].astype(low)
+        for t in range(3):
+            part[pl.ds(base + (t + 1) * 768, 768), :] = dot(ln1_ref[...], d_ref[t], 0, 0).astype(low)
+        comm.start(1, 2 * tiles + 2 * p)
+        comm.start(1, 2 * tiles + 2 * p + 1)
+        for t in range(3):
+            for part_rows in range(2):
+                chunk = slice(part_rows * own_rows, (part_rows + 1) * own_rows)
+                acc0[chunk, :] += dot(d_ref[t, chunk, :], qkvw_ref[t, :, lanes], 1, 1)
+        small[pl.ds(24 + p, 1), :] = column_sum(d_ref[0].astype(f32))
+        small[pl.ds(27 + p, 1), :] = column_sum(d_ref[2].astype(f32))
+        return carry
+
+    lax.fori_loop(0, pairs, pair_step, 0)
+    send_dn = pair_copy(acc0.at[away], land1, 3)
+    send_dn.start()
+    tokens = tok_ref[...].astype(f32)
+    centred = tokens - jnp.mean(tokens, axis=-1, keepdims=True)
+    inv_std = lax.rsqrt(jnp.mean(centred * centred, axis=-1, keepdims=True) + EPSILON)
+    normal = centred * inv_std
+    send_dn.wait_recv()
+    grad_norm = acc0[own, :] + land1[...]
+    put_vector(small, 0, column_sum(grad_norm * normal))
+    put_vector(small, 6, column_sum(grad_norm))
+    input_out[...] = (gresid[...] + norm_back(grad_norm, normal, inv_std, gain1[0:1, :].astype(f32))).astype(low)
+    send_dn.wait_send()
+    send_cot.wait_send()
+    sm = small_sum(comm, small, small_out, land_c, land_x, land_y, land_z, sacc, ss, sr)
+    next(sm)
+    first = tiles - LAG + 3 * pairs
+    last = n + 5
+    for mark in range(4):
+        lax.fori_loop(first + mark * (last - first) // 4, first + (mark + 1) * (last - first) // 4,
+                      lambda w, c: (wave(w), c)[1], 0)
+        next(sm)
+    lax.fori_loop(0, n, lambda i, c: (comm.sent(i), c)[1], 0)
+
+
+def back_call(x, g, fc_weight, fc_bias, proj_weight, proj_bias, gain1, gain2, out_weight, qkv_weight, projected, lse,
+              mixed, ln1_full, residual, tokens):
     rows, depth = x.shape
     units = fc_weight.shape[1]
-    tiles = units // UNITS
-    f32, low = jnp.float32, jnp.bfloat16
-    whole = pl.BlockSpec((rows, depth), lambda i: (0, 0))
-    item = pl.BlockSpec((ITEM, 128), lambda i: (i, 0))
+    width = out_weight.shape[0]
+    tiles, pairs = units // UNITS, width // 128
+    n = 2 * tiles + 2 * pairs
+    f32, bf = jnp.float32, jnp.bfloat16
+    near, far = pl.BlockSpec(memory_space=pltpu.VMEM), pl.BlockSpec(memory_space=pl.ANY)
+    late = [fc_weight, proj_weight, out_weight, qkv_weight, projected, lse, mixed, ln1_full, residual, tokens]
+    own_rows = rows // 2
+    dma = pltpu.SemaphoreType.DMA
     return pl.pallas_call(
-        mlp_kernel,
-        grid=(tiles,),
-        out_shape=(jax.ShapeDtypeStruct((rows, depth), f32), jax.ShapeDtypeStruct((rows, depth), f32),
-                   jax.ShapeDtypeStruct((tiles * ITEM, 128), low), jax.ShapeDtypeStruct((tiles * ITEM, 128), low),
-                   jax.ShapeDtypeStruct((1, units), f32), jax.ShapeDtypeStruct((1, depth), f32)),
-        in_specs=[whole, whole, pl.BlockSpec((depth, UNITS), lambda i: (0, i)),
-                  pl.BlockSpec((1, UNITS), lambda i: (0, i)), pl.BlockSpec((UNITS, depth), lambda i: (i, 0))],
-        out_specs=(whole, whole, item, item, pl.BlockSpec((1, UNITS), lambda i: (0, i)),
-                   pl.BlockSpec((1, depth), lambda i: (0, 0))),
-        compiler_params=pltpu.CompilerParams(vmem_limit_bytes=60 * 2**20),
-        cost_estimate=pl.CostEstimate(flops=17 * 10**9, bytes_accessed=25 * 10**6, transcendentals=2 * 10**6),
-        name="mlp",
-    )(x, g, fc_weight, fc_bias.reshape(1, units), proj_weight)
+        functools.partial(back_kernel, n, tiles, pairs),
+        out_shape=(jax.ShapeDtypeStruct((n * ITEM, 128), bf), jax.ShapeDtypeStruct((SMALL, 128), f32),
+                   jax.ShapeDtypeStruct((own_rows, depth), bf), jax.ShapeDtypeStruct((own_rows, depth), bf)),
+        in_specs=[near, near, far, near, far, near, near, near] + [far] * 8,
+        out_specs=(far, near, near, near),
+        scratch_shapes=[pltpu.VMEM(a.shape, a.dtype) for a in late] + [dma((10,))] + [
+            pltpu.VMEM((rows, UNITS), bf), pltpu.VMEM((rows, UNITS), bf),
+            pltpu.VMEM((rows, depth), f32), pltpu.VMEM((rows, depth), f32),
+            pltpu.VMEM((own_rows, depth), f32), pltpu.VMEM((own_rows, depth), f32),
+            pltpu.VMEM((rows, depth), bf), pltpu.VMEM((own_rows, depth), f32),
+            pltpu.VMEM((rows, 128), bf)] + [pltpu.VMEM((rows, 128), f32)] * 3 + [
+            pltpu.VMEM((3, rows, 128), bf),
+            pltpu.VMEM((n * ITEM, 128), bf),
+            pltpu.VMEM((n * ITEM // 2, 128), bf),
+            pltpu.VMEM((n * ITEM // 4, 128), bf),
+            pltpu.VMEM((n * 3 * ITEM // 16, 128), bf),
+            dma((10, n)), dma((10, n)), dma((n,)), dma((4,)), dma((4,)),
+            pltpu.VMEM((SMALL, 128), f32),
+            pltpu.VMEM((LN_ROWS, 128), f32),
+            pltpu.VMEM((SMALL, 128), f32),
+            pltpu.VMEM((SMALL, 128), f32),
+            pltpu.VMEM((4, SMALL, 128), f32),
+            pltpu.VMEM((3, SMALL, 128), f32),
+            dma((6,)), dma((6,)),
+        ],
+        compiler_params=pltpu.CompilerParams(
+            collective_id=0, has_side_effects=True, vmem_limit_bytes=67043328),
+        cost_estimate=pl.CostEstimate(flops=30 * 10**9, bytes_accessed=40 * 10**6, transcendentals=6 * 10**6),
+        name="back",
+    )(x, g, fc_weight, fc_bias.reshape(1, units), proj_weight, proj_bias.reshape(1, depth),
+      gain1.reshape(1, depth), gain2.reshape(1, depth), out_weight, qkv_weight, projected, lse, mixed, ln1_full,
+      residual, tokens)
 
 
 def spread_kernel(p_ref, f_ref, proj_ref, fc_ref):
@@ -498,8 +555,8 @@
         spread_kernel,
         grid=(tiles,),
         out_shape=(jax.ShapeDtypeStruct((units, depth), f32), jax.ShapeDtypeStruct((depth, units), f32)),
-        in_specs=[pl.BlockSpec((ITEM, 128), lambda i: (i, 0)),
-                  pl.BlockSpec((ITEM, 128), lambda i: (i + tiles, 0))],
+        in_specs=[pl.BlockSpec((ITEM, 128), lambda i: (2 * i, 0)),
+                  pl.BlockSpec((ITEM, 128), lambda i: (2 * i + 1, 0))],
         out_specs=(pl.BlockSpec((UNITS, depth), lambda i: (i, 0)), pl.BlockSpec((depth, UNITS), lambda i: (0, i))),
         compiler_params=pltpu.CompilerParams(vmem_limit_bytes=24 * 2**20),
         name="spread_mlp",
@@ -573,41 +630,12 @@
     normed2, normal2, inv_std2 = norm_rows(residual, gain_two, ln2_bias.astype(jnp.float32))
     ln2_full = gather_pair(normed2.astype(jnp.bfloat16))
     cot_full = gather_pair(cotangent)
-    mlp_part, norm2_part, part_proj, part_fc, grad_fc_bias, grad_proj_bias = mlp_call(
-        ln2_full, cot_full, fc_weight, fc_bias, proj_weight
-    )
-    block_output = (residual + (scatter_pair(mlp_part) + proj_bias.astype(jnp.float32))).astype(jnp.bfloat16)
-    grad_norm2 = scatter_pair(norm2_part)
-    grad_resid = cotangent.astype(jnp.float32) + norm_back(grad_norm2, normal2, inv_std2, gain_two)
-    part_ln2_gain = jnp.sum(grad_norm2 * normal2, axis=0)
-    part_ln2_bias = jnp.sum(grad_norm2, axis=0)
-    attn_cot_full = gather_pair(grad_resid.astype(jnp.bfloat16))
-    part_attn, norm1_part, grad_bias_rows, grad_out_bias = attend_back_call(
-        projected, lse, mixed_low, attn_cot_full, ln1_full, out_weight, qkv_weight
-    )
-    grad_norm1 = scatter_pair(norm1_part)
-    input_grad = (grad_resid + norm_back(grad_norm1, normal1, inv_std1, gain_one)).astype(
-        jnp.bfloat16
-    )
-    part_ln1_gain = jnp.sum(grad_norm1 * normal1, axis=0)
-    part_ln1_bias = jnp.sum(grad_norm1, axis=0)
     width = tokens.shape[1]
     units = fc_weight.shape[1]
-    small = jnp.concatenate(
-        [
-            part_ln1_gain,
-            part_ln1_bias,
-            part_ln2_gain,
-            part_ln2_bias,
-            grad_bias_rows[0],
-            grad_bias_rows[2],
-            grad_out_bias[0],
-            grad_fc_bias[0],
-            grad_proj_bias[0],
-            jnp.zeros((SMALL * 128 - 6912,), jnp.float32),
-        ]
-    ).reshape(SMALL, 128)
-    total, small = sum_call((part_proj, part_fc, part_attn), small)
+    total, small, block_output, input_grad = back_call(
+        ln2_full, cot_full, fc_weight, fc_bias, proj_weight, proj_bias, ln1_gain, ln2_gain, out_weight, qkv_weight,
+        projected, lse, mixed_low, ln1_full, residual, tokens
+    )
     grad_proj_weight, grad_fc_weight = spread_call(total, units, width)
     grad_out_weight, grad_qkv_weight = spread_pair_call(
         total, 2 * units * width // 128, local_width, width

time: 307 us -> 223 us (0.73)
  Pallas kernels: 248 us -> 189 us
  waiting for transfers between devices: 14.5 us -> 3.54 us
  other arithmetic: 16 us -> 5.52 us
    pallas_call x3 -> x1, Pallas kernels: 218 us -> 159 us  [back_call(): pl.pallas_call(functools.partial(back_kernel, n, tiles, pairs), out_shape...]
    ppermute x8 -> x4, waiting for transfers between devices: 14.5 us -> 3.54 us  [swap(): return lax.ppermute(values, 'tensor', [(0, 1), (1, 0)])]
    reduce_sum x2 -> x0, other arithmetic: 5.34 us -> none  [the longest x1 3.38 us: on_device(): part_ln1_gain = jnp.sum(grad_norm1 * normal1, axis=0)]
    dynamic_slice x4 -> x1, local copies, waits for them, and re-layouts: 4.81 us -> 0.12 us  [scatter_pair(): away = lax.dynamic_slice_in_dim(part, (1 - t) * rows, rows, 0)]
    unnamed x75 -> x44, local copies, waits for them, and re-layouts: 6.55 us -> 5.96 us
  transfers between devices with their start and end apart: 8 -> 4, of which waited for: 6 -> 2; matrix products, arithmetic and copies ran while one was open for 3% -> 4% of each run, Pallas kernels for 0% -> 0%
where the time goes in v3:
time: 223 us
  Pallas kernels  189 us (85%)
  local copies, waits for them, and re-layouts  18.1 us (8%)
  other arithmetic  5.52 us (2%)
  waiting for transfers between devices  3.54 us (2%)
  matrix products  3.54 us (2%)
    pallas_call x1, Pallas kernels, back_call(): pl.pallas_call(functools.partial(back_kernel, n, tiles, pairs), out_shape...  159 us
    pallas_call x1, Pallas kernels, attend_call(): pl.pallas_call(attend_kernel, grid=(pairs,), out_shape=(jax.ShapeDtypeStr...  23.5 us
    unnamed x44, local copies, waits for them, and re-layouts  5.96 us
  transfers between devices with their start and end apart: 4, of which 2 were waited for; matrix products, arithmetic and copies ran while one was open for 4% of the time, Pallas kernels for 0%

profile of v3, /device:TPU:0, one launch (start us, length us, event | category | flops | bytes accessed | tf_op | source)
XLA Modules:
  0.0 222.7 jit_solution(15395542956356381384)
XLA Ops:
  0.6 0.0 copy-start.12
  0.7 0.0 copy-start.5
  0.7 1.4 convert_reduce_fusion
  2.1 1.6 fusion.3
  3.8 0.1 broadcast.50.clone.1
  3.9 0.4 constant_dynamic-update-slice_fusion.5
  4.3 0.6 collective-permute-start
  4.9 0.1 pad.1.clone
  4.9 0.8 fusion.10
  5.8 0.1 pad_maximum_fusion
  5.8 1.2 collective-permute-done
  7.0 1.2 constant_dynamic-update-slice_fusion.4.refs_13_
  8.3 2.5 %fusion.q_ref.k_ref.v_ref.refs_10_ = bf16[3,1152,384]{2,1,0:T(8,128)(2,1)S(1)} fusion(bf16[3,768,384]{2,1,0:T(8,128)(2,1)S(1)} %copy-done.20, f32[3,384]{1,0:T(4,128)S(1)} %pad_maximum_fusion, bf16[1152,768]{1,0:T(8,128)(2,1)S(1)} %constant_dynamic-update-slice_fusion.4.refs_13_), kind=kOutput, calls=%fused_computation.1 | convolution fusion | flops 2041085952 | bytes 6197760 | tf_op jit(solution)/shard_map/gd,tdj->tgj/dot_general | solution.py:622
  10.8 0.0 copy-start.2
  10.8 0.0 copy-start.10
  10.8 23.5 %attend.1 = (bf16[1152,384]{1,0:T(8,128)(2,1)S(1)}, f32[1152,384]{1,0:T(8,128)S(1)}) custom-call(bf16[3,1152,384]{2,1,0:T(8,128)(2,1)S(1)} %fusion.q_ref.k_ref.v_ref.refs_10_, bf16[3,1152,384]{2,1,0:T(8,128)(2,1)S(1)} %fusion.q_ref.k_ref.v_ref.refs_10_, bf16[3,1152,384]{2,1,0:T(8,128)(2,1)S(1)} %fusion.q_ref.k_ref.v_ref.refs_10_), custom_call_target="tpu_custom_call" | custom-call | flops 4000000000 | bytes 6000000 | tf_op jit(solution)/shard_map/attend/pallas_call | solution.py:265
  34.3 0.0 copy-start.1
  34.3 1.1 fusion.11
  35.4 0.5 copy-done.3
  35.9 0.1 constant_dynamic-slice_fusion
  36.0 0.4 collective-permute-start.1
  36.5 0.6 copy-done.9
  37.1 0.4 collective-permute-start.3
  37.5 2.3 %collective-permute-done.1 = f32[576,768]{1,0:T(8,128)S(1)} collective-permute-done((f32[576,768]{1,0:T(8,128)S(1)}, f32[576,768]{1,0:T(8,128)S(1)}, u32[]{:S(2)}, u32[]{:S(2)}) %collective-permute-start.1) | collective-permute-done | bytes 1769504 | tf_op jit(solution)/shard_map/ppermute | solution.py:186
  39.8 0.4 fusion.8
  40.2 0.3 multiply_reduce_fusion
  40.5 1.4 broadcast.50.clone
  42.0 1.3 constant_dynamic-update-slice_fusion.3
  43.2 0.4 collective-permute-start.2
  43.6 0.6 reshape.85.refs_6_
  44.2 0.6 reshape.86.refs_7_
  44.8 0.6 reshape.83.refs_3_
  45.4 0.6 reshape.84.refs_5_
  46.0 1.3 broadcast.50.clone.2
  47.3 1.0 constant_dynamic-update-slice_fusion.1
  48.3 0.0 collective-permute-done.3
  48.3 1.0 constant_dynamic-update-slice_fusion.refs_1_
  49.2 0.0 collective-permute-done.2
  49.2 1.0 constant_dynamic-update-slice_fusion.2.refs_0_
  50.2 159.3 %back.1 = (bf16[27648,128]{1,0:T(8,128)(2,1)}, f32[56,128]{1,0:T(8,128)}, bf16[576,768]{1,0:T(8,128)(2,1)}, bf16[576,768]{1,0:T(8,128)(2,1)}) custom-call(bf16[1152,768]{1,0:T(8,128)(2,1)} %constant_dynamic-update-slice_fusion.2.refs_0_, bf16[1152,768]{1,0:T(8,128)(2,1)} %constant_dynamic-update-slice_fusion.refs_1_, bf16[768,1536]{1,0:T(8,128)(2,1)} %refs_2_.1, ...), custom_call_target="tpu_custom_call" | custom-call | flops 30000001024 | bytes 40000000 | tf_op jit(solution)/shard_map/back/pallas_call | solution.py:508
  209.5 3.0 %copy-done = bf16[27648,128]{1,0:T(8,128)(2,1)S(1)} copy-done((bf16[27648,128]{1,0:T(8,128)(2,1)S(1)}, bf16[27648,128]{1,0:T(8,128)(2,1)}, u32[]{:S(2)}) %copy-start) | copy-done | bytes 7077912
  212.5 4.1 %spread_mlp.1 = (f32[1536,768]{1,0:T(8,128)}, f32[768,1536]{1,0:T(8,128)}) custom-call(bf16[27648,128]{1,0:T(8,128)(2,1)S(1)} %copy-done, bf16[27648,128]{1,0:T(8,128)(2,1)S(1)} %copy-done), custom_call_target="tpu_custom_call" | custom-call | tf_op jit(solution)/shard_map/spread_mlp/pallas_call | solution.py:554
  216.6 2.4 %spread_attend.1 = (f32[384,768]{1,0:T(8,128)}, f32[3,768,384]{2,1,0:T(8,128)}) custom-call(bf16[27648,128]{1,0:T(8,128)(2,1)S(1)} %copy-done), custom_call_target="tpu_custom_call" | custom-call | tf_op jit(solution)/shard_map/spread_attend/pallas_call | solution.py:578
  219.1 0.6 slice_bitcast_fusion.1
  219.7 0.6 slice_bitcast_fusion
  220.3 0.6 reshape.87
  220.9 0.9 copy.36
  221.8 0.9 copy.37
  (43 shorter events, 0.1 us)
Async XLA Ops:
  0.6 3.1 %copy-start.12 = (bf16[768]{0:T(1024)(128)(2,1)S(1)}, bf16[768]{0:T(1024)(128)(2,1)}, u32[]{:S(2)}) copy-start(bf16[768]{0:T(1024)(128)(2,1)} %param.15) | copy-start | bytes 4612
  0.7 3.1 %copy-start.16 = (bf16[768]{0:T(1024)(128)(2,1)S(1)}, bf16[768]{0:T(1024)(128)(2,1)}, u32[]{:S(2)}) copy-start(bf16[768]{0:T(1024)(128)(2,1)} %param.16) | copy-start | bytes 4612
  0.7 3.2 %copy-start.5 = (bf16[576,768]{1,0:T(8,128)(2,1)S(1)}, bf16[576,768]{1,0:T(8,128)(2,1)}, u32[]{:S(2)}) copy-start(bf16[576,768]{1,0:T(8,128)(2,1)} %refs_15_.1) | copy-start | bytes 2654212
  4.3 2.7 %collective-permute-start = (bf16[576,768]{1,0:T(8,128)(2,1)S(1)}, bf16[576,768]{1,0:T(8,128)(2,1)}, u32[]{:S(2)}, u32[]{:S(2)}) collective-permute-start(bf16[576,768]{1,0:T(8,128)(2,1)S(1)} %get-tuple-element.39), channel_id=1, source_target_pairs={{0,1},{1,0},{2,3},{3,2},{4,5},{5,4},{6,7},{7,6},{8,9},{9,8},{10,11... | collective-permute-start | bytes 2654216 | tf_op jit(solution)/shard_map/ppermute | solution.py:186
  4.9 3.4 %copy-start.20 = (bf16[3,768,384]{2,1,0:T(8,128)(2,1)S(1)}, bf16[3,768,384]{2,1,0:T(8,128)(2,1)}, u32[]{:S(2)}) copy-start(bf16[3,768,384]{2,1,0:T(8,128)(2,1)} %refs_9_.1) | copy-start | bytes 5308420
  8.3 2.5 %copy-start.6 = (bf16[1152,768]{1,0:T(8,128)(2,1)}, bf16[1152,768]{1,0:T(8,128)(2,1)S(1)}, u32[]{:S(2)}) copy-start(bf16[1152,768]{1,0:T(8,128)(2,1)S(1)} %constant_dynamic-update-slice_fusion.4.refs_13_) | copy-start | bytes 5308420
  10.8 23.5 %copy-start.2 = (bf16[3,1152,384]{2,1,0:T(8,128)(2,1)}, bf16[3,1152,384]{2,1,0:T(8,128)(2,1)S(1)}, u32[]{:S(2)}) copy-start(bf16[3,1152,384]{2,1,0:T(8,128)(2,1)S(1)} %fusion.q_ref.k_ref.v_ref.refs_10_) | copy-start | bytes 7962628
  10.8 23.5 %copy-start.10 = (bf16[384,768]{1,0:T(8,128)(2,1)S(1)}, bf16[384,768]{1,0:T(8,128)(2,1)}, u32[]{:S(2)}) copy-start(bf16[384,768]{1,0:T(8,128)(2,1)} %refs_8_.1) | copy-start | bytes 1769476
  34.3 1.1 copy-start.1
  34.3 1.6 copy-start.3
  35.9 1.2 copy-start.9
  35.9 1.5 copy-start.17
  35.9 1.5 copy-start.14
  35.9 1.6 copy-start.18
  36.0 3.8 %collective-permute-start.1 = (f32[576,768]{1,0:T(8,128)S(1)}, f32[576,768]{1,0:T(8,128)S(1)}, u32[]{:S(2)}, u32[]{:S(2)}) collective-permute-start(f32[576,768]{1,0:T(8,128)S(1)} %constant_dynamic-slice_fusion), channel_id=1, source_target_pairs={{0,1},{1,0},{2,3},{3,2},{4,5},{5,4},{6,7},{7,6},{8,9},{9,8},{10,11... | collective-permute-start | bytes 5308424 | tf_op jit(solution)/shard_map/ppermute | solution.py:186
  37.1 11.2 %collective-permute-start.3 = (bf16[576,768]{1,0:T(8,128)(2,1)S(1)}, bf16[576,768]{1,0:T(8,128)(2,1)S(1)}, u32[]{:S(2)}, u32[]{:S(2)}) collective-permute-start(bf16[576,768]{1,0:T(8,128)(2,1)S(1)} %copy-done.9), channel_id=1, source_target_pairs={{0,1},{1,0},{2,3},{3,2},{4,5},{5,4},{6,7},{7,6},{8,9},{9,8},{10,11... | collective-permute-start | bytes 2654216 | tf_op jit(solution)/shard_map/ppermute | solution.py:186
  40.2 1.8 copy-start.4
  42.0 1.7 copy-start.13
  42.0 2.8 %copy-start.15 = (bf16[1536]{0:T(1024)(128)(2,1)S(1)}, bf16[1536]{0:T(1024)(128)(2,1)}, u32[]{:S(2)}) copy-start(bf16[1536]{0:T(1024)(128)(2,1)} %param.24) | copy-start | bytes 9220
  42.0 3.4 %copy-start.19 = (bf16[768]{0:T(1024)(128)(2,1)S(1)}, bf16[768]{0:T(1024)(128)(2,1)}, u32[]{:S(2)}) copy-start(bf16[768]{0:T(1024)(128)(2,1)} %param.26) | copy-start | bytes 4612
  43.2 6.0 %collective-permute-start.2 = (bf16[576,768]{1,0:T(8,128)(2,1)S(1)}, bf16[576,768]{1,0:T(8,128)(2,1)S(1)}, u32[]{:S(2)}, u32[]{:S(2)}) collective-permute-start(bf16[576,768]{1,0:T(8,128)(2,1)S(1)} %get-tuple-element.35), channel_id=1, source_target_pairs={{0,1},{1,0},{2,3},{3,2},{4,5},{5,4},{6,7},{7,6},{8,9},{9,8},{10,11... | collective-permute-start | bytes 2654216 | tf_op jit(solution)/shard_map/ppermute | solution.py:186
  209.5 3.0 %copy-start = (bf16[27648,128]{1,0:T(8,128)(2,1)S(1)}, bf16[27648,128]{1,0:T(8,128)(2,1)}, u32[]{:S(2)}) copy-start(bf16[27648,128]{1,0:T(8,128)(2,1)} %get-tuple-element.29.a_ref.p_ref.f_ref) | copy-start | bytes 21233668
  216.6 2.5 %copy-start.11 = (f32[56,128]{1,0:T(8,128)S(1)}, f32[56,128]{1,0:T(8,128)}, u32[]{:S(2)}) copy-start(f32[56,128]{1,0:T(8,128)} %get-tuple-element.28) | copy-start | bytes 86020
  216.6 4.3 %copy-start.8 = (bf16[576,768]{1,0:T(8,128)(2,1)S(1)}, bf16[576,768]{1,0:T(8,128)(2,1)}, u32[]{:S(2)}) copy-start(bf16[576,768]{1,0:T(8,128)(2,1)} %get-tuple-element.63) | copy-start | bytes 2654212
  219.0 2.7 %copy-start.7 = (bf16[576,768]{1,0:T(8,128)(2,1)S(1)}, bf16[576,768]{1,0:T(8,128)(2,1)}, u32[]{:S(2)}) copy-start(bf16[576,768]{1,0:T(8,128)(2,1)} %get-tuple-element.64) | copy-start | bytes 2654212
